TPU v7x, 256 devices: a whole 4x4x8 slice. The times are simulated.
256 devices in a mesh: dp: 32 (over x, z), tensor: 8 (over y, core).
Axes of the slice: x: 4, y: 4, z: 8, core: 2. Of those that a mesh axis runs over, the one named last changes fastest.
Arguments:
- vis_rows: bfloat16 [8, 256, 2, 3200], P(None, 'dp', None, 'tensor'), may hold values from -6 to 6
- ln_gain: float32 [2, 3200], replicated, may hold values from 0.25 to 1.75
- ln_bias: float32 [2, 3200], replicated, may hold values from -3 to 3
- proj_weight: bfloat16 [3200, 2, 8192], P('dp', None, 'tensor'), may hold values from -0.078125 to 0.078125
- text_rows: bfloat16 [32, 384, 8192], P('dp', None, 'tensor'), may hold values from -8 to 8
- attn_gain: float32 [8192], replicated, may hold values from 0.25 to 1.75
- w_query: bfloat16 [8192, 4096], P('dp', 'tensor'), may hold values from -0.088388348 to 0.088388348
- key_value_weight: bfloat16 [8192, 2, 1024], P('dp', None, 'tensor'), may hold values from -0.088388348 to 0.088388348
- tile_counts: int32 [32], replicated, may hold values from 1 to 16, 256 in all
- image_offsets: int32 [32], P('dp'), may hold values from 0 to 256
Outputs:
- attn_context: bfloat16 [32, 384, 4096], P('dp', None, 'tensor')
Inputs may be any that keep to these rules, and one draw needn't show every extreme that they name: tile_counts counts all 256 tiles, and its largest entry is exactly 16.
All inputs are finite; a program needn't handle non-finite values.
Results may differ from a plain program's by a relative error of at most 0.0074.
Values may be sent and summed in bfloat16 or wider, within the bound.
A program may use at most 128 MiB of HBM per device.

v0:
```python
import jax
import jax.numpy as jnp
from jax import lax
from jax.sharding import PartitionSpec as P

QUERY_HEADS = 32
KEY_VALUE_HEADS = 8
HEAD_WIDTH = 128


vision_epsilon = 1e-06
decoder_epsilon = 1e-05
rope_base = 500000.0


def from_everyone(array, axis):
    count = lax.axis_size(axis)
    return lax.all_to_all(
        jnp.broadcast_to(array[None], (count, *array.shape)), axis, 0, 0, tiled=True
    )


def laid_out(tiles, dim):
    shape = list(tiles.shape[1:])
    shape[dim] *= tiles.shape[0]
    return jnp.moveaxis(tiles, 0, dim).reshape(shape)


def gather_directly(array, axis, dim):
    tiles = from_everyone(array, axis)
    return laid_out(tiles, dim)


def sent_together(arrays, axis, dim, along):
    columns = [a.reshape(*a.shape[:along], -1) for a in arrays]
    both = jnp.concatenate(columns, axis=along)
    filled, at, finished = (lax.all_gather(both, axis, axis=dim, tiled=True), 0, [])
    for a, column in zip(arrays, columns):
        piece = filled[..., at : at + column.shape[along]]
        finished.append(piece.reshape(*piece.shape[:along], *a.shape[along:]))
        at += column.shape[along]
    return tuple(finished)


def apply_rotary(value_rows, position_indices):
    half_width = value_rows.shape[-1] // 2
    exponents = jnp.arange(half_width, dtype=jnp.float32) * (2.0 / value_rows.shape[-1])
    frequency = rope_base ** (-exponents)
    angles = position_indices.astype(jnp.float32)[:, None] * frequency[None, :]
    cosine = jnp.cos(angles)[:, None, :]
    sine = jnp.sin(angles)[:, None, :]
    first_half = value_rows[..., :half_width]
    second_half = value_rows[..., half_width:]
    return jnp.concatenate(
        [first_half * cosine - second_half * sine, second_half * cosine + first_half * sine],
        axis=-1,
    )


def layer_norm(value_rows, gain, bias_values):
    average = jnp.mean(value_rows, axis=(-2, -1), keepdims=True)
    centered = value_rows - average
    variance = jnp.mean(centered * centered, axis=(-2, -1), keepdims=True)
    return centered * lax.rsqrt(variance + vision_epsilon) * gain + bias_values


def attend(query_full, key_value_complete):
    seq_len = query_full.shape[0]
    query_group_count = QUERY_HEADS // KEY_VALUE_HEADS
    local_kv = key_value_complete.shape[2] // HEAD_WIDTH
    local_query = query_full.shape[1] // HEAD_WIDTH
    position_indices = jnp.arange(seq_len, dtype=jnp.int32)
    query_rows = apply_rotary(
        query_full.reshape(seq_len, local_query, HEAD_WIDTH), position_indices
    ).astype(jnp.bfloat16)
    query_rows = query_rows.reshape(seq_len, local_kv, query_group_count, HEAD_WIDTH)
    key_rows = apply_rotary(
        key_value_complete[:, 0].reshape(seq_len, local_kv, HEAD_WIDTH), position_indices
    ).astype(jnp.bfloat16)
    value_rows = (
        key_value_complete[:, 1].reshape(seq_len, local_kv, HEAD_WIDTH).astype(jnp.bfloat16)
    )
    scores = jnp.einsum(
        "pgjd,kgd->gjpk", query_rows, key_rows, preferred_element_type=jnp.float32
    ) * HEAD_WIDTH ** (-0.5)
    causal = position_indices[:, None] >= position_indices[None, :]
    scores = jnp.where(causal[None, None], scores, -1e30)
    row_max = jnp.max(scores, axis=-1, keepdims=True)
    exponentials = jnp.exp(scores - row_max)
    weights = (exponentials / jnp.sum(exponentials, axis=-1, keepdims=True)).astype(jnp.bfloat16)
    context = jnp.einsum("gjpk,kgd->pgjd", weights, value_rows, preferred_element_type=jnp.float32)
    return context.astype(jnp.bfloat16).reshape(seq_len, local_query * HEAD_WIDTH)


def per_device(
    vis_rows,
    ln_gain,
    ln_bias,
    proj_weight,
    text_rows,
    attn_gain,
    w_query,
    key_value_weight,
    tile_counts,
    image_offsets,
):
    data_count = lax.axis_size("dp")
    data_index = lax.axis_index("dp")
    tile_rows, tile_tok, merge_count, part_width = vis_rows.shape
    vision_width = ln_gain.shape[1]
    part_model = proj_weight.shape[2]
    token_count = tile_rows * tile_tok
    max_tiles = 2 * tile_rows
    slot_count = (max_tiles + data_count - 1) // data_count
    tile_ends = jnp.cumsum(tile_counts)
    tile_firsts = tile_ends - tile_counts
    sample_ids = jnp.arange(data_count, dtype=jnp.int32)
    tiles_here = jnp.arange(tile_rows, dtype=jnp.int32) * data_count + data_index
    owners = jnp.sum((tile_ends[None, :] <= tiles_here[:, None]).astype(jnp.int32), axis=1)
    owner_first = jnp.sum(
        jnp.where(sample_ids[None, :] == owners[:, None], tile_firsts[None, :], 0), axis=1
    )
    slots = (tiles_here - owner_first) // data_count
    is_mine = sample_ids == data_index
    my_first = jnp.sum(jnp.where(is_mine, tile_firsts, 0))
    my_count = jnp.sum(jnp.where(is_mine, tile_counts, 0))
    tile_order = jnp.arange(max_tiles, dtype=jnp.int32)
    sources = (my_first + tile_order) % data_count
    slot_index = tile_order // data_count
    image_span = max_tiles * tile_tok
    whole = gather_directly(vis_rows, "tensor", 3)
    merged = whole.reshape(token_count, merge_count, vision_width).astype(jnp.float32)
    normed_vis = layer_norm(merged, ln_gain, ln_bias).astype(jnp.bfloat16)
    columns = normed_vis
    image_cols = (
        jnp.einsum(
            "rmf,fmo->ro",
            columns,
            lax.all_gather(proj_weight, "dp", axis=0, tiled=True),
            preferred_element_type=jnp.float32,
        )
        .astype(jnp.bfloat16)
        .reshape(tile_rows, tile_tok, part_model)
    )
    empty_slots = jnp.zeros((data_count, slot_count) + image_cols.shape[1:], jnp.bfloat16)
    received = lax.all_to_all(
        empty_slots.at[owners, slots].set(image_cols), "dp", split_axis=0, concat_axis=0, tiled=True
    )
    arrived = received[sources, slot_index]
    arrived = arrived.reshape(image_span, part_model)
    start_row = image_offsets[0]
    sequence = text_rows[0]
    current = lax.dynamic_slice_in_dim(sequence, start_row, image_span, 0)
    is_image = jnp.repeat(tile_order < my_count, tile_tok)[:, None]
    combined = jnp.where(is_image, arrived, current)
    sequence = lax.dynamic_update_slice_in_dim(sequence, combined, start_row, 0)
    gathered = gather_directly(sequence, "tensor", 1)
    seq_float = gathered.astype(jnp.float32)
    mean_square = jnp.mean(seq_float * seq_float, axis=-1, keepdims=True)
    normalized_sequence = (seq_float * lax.rsqrt(mean_square + decoder_epsilon) * attn_gain).astype(
        jnp.bfloat16
    )
    seq_len = normalized_sequence.shape[0]
    weight_rows = sent_together((w_query, key_value_weight), "dp", 0, 1)
    columns = normalized_sequence
    query_part = jnp.dot(columns, weight_rows[0], preferred_element_type=jnp.float32)
    keyval_part = jnp.einsum(
        "sd,dck->sck", columns, weight_rows[1], preferred_element_type=jnp.float32
    )
    context = attend(query_part, keyval_part)
    return context.reshape(1, seq_len, context.shape[1])


def solution(mesh):
    in_specs = (
        P(None, "dp", None, "tensor"),
        P(),
        P(),
        P("dp", None, "tensor"),
        P("dp", None, "tensor"),
        P(),
        P("dp", "tensor"),
        P("dp", None, "tensor"),
        P(),
        P("dp"),
    )
    out_specs = P("dp", None, "tensor")
    return jax.shard_map(
        per_device, mesh=mesh, in_specs=in_specs, out_specs=out_specs, check_vma=False
    )
```

profile of v0, /device:TPU:8, one launch (start us, length us, event | category | flops | bytes accessed | tf_op | source)
XLA Modules:
  0.0 314.5 jit_solution(18428205670531530554)
XLA Ops:
  6.5 1.2 copy.86
  7.8 0.9 copy.81
  8.7 0.8 pad_maximum_fusion
  9.6 1.1 broadcast_in_dim.55
  10.7 5.6 %all-to-all-start = ((bf16[8,8,8,2,400]{4,2,1,3,0:T(8,128)(2,1)}), bf16[8,8,8,2,400]{4,2,1,3,0:T(8,128)(2,1)S(1)}, u32[]{:S(2)}, u32[]{:S(2)}) async-start(bf16[8,8,8,2,400]{4,2,1,3,0:T(8,128)(2,1)} %broadcast_in_dim.55), calls=%async_computation | async-start | bytes 2097152 | tf_op jit(solution)/shard_map/all_to_all | solution.py:18
  16.8 0.7 fusion.48
  17.7 13.1 %all-to-all-done = bf16[8,8,8,2,400]{4,2,1,3,0:T(8,128)(2,1)S(1)} async-done(((bf16[8,8,8,2,400]{4,2,1,3,0:T(8,128)(2,1)}), bf16[8,8,8,2,400]{4,2,1,3,0:T(8,128)(2,1)S(1)}, u32[]{:S(2)}, u32[]{:S(2)}) %all-to-all-start) | async-done | bytes 819232 | tf_op jit(solution)/shard_map/all_to_all | solution.py:18
  32.0 1.6 copy.53
  33.7 2.3 reshape.465
  36.0 98.4 %all-gather.3.cloned.1.call-done = bf16[3200,2,1024]{2,1,0:T(2,128)(2,1)} async-done(((bf16[100,2,1024]{2,1,0:T(2,128)(2,1)}), bf16[3200,2,1024]{2,1,0:T(2,128)(2,1)}) %all-gather.3.cloned.1.call-update) | async-done | bytes 13107216 | tf_op jit(solution)/shard_map/all_gather | solution.py:139
  134.4 9.4 %fusion.16 = bf16[8,8,1024]{2,1,0:T(8,128)(2,1)S(1)} fusion(bf16[3200,2,1024]{2,1,0:T(2,128)(2,1)} %all-gather.3.cloned.1.call-done, f32[64,2,3200]{2,0,1:T(8,128)} %reshape.465, f32[2,3200]{1,0:T(2,128)S(1)} %copy-done.5, f32[2,3200]{1,0:T(2,128)S(1)} %copy-done.6, f32[64]{0:T(128)S(1)} %rsqrt.20, f32[64]{0:T(128)S(1)} %div.47), kind=kOutput, calls=%fused_computation.24 | convolution fusion | flops 840974336 | bytes 14928384 | tf_op jit(solution)/shard_map/rmf,fmo->ro/dot_general | solution.py:136
  143.8 0.9 broadcast.417
  144.7 2.1 scatter_fusion
  146.8 5.6 %all-to-all-start.1 = ((bf16[32,1,8,1024]{3,2,1,0:T(8,128)(2,1)}), bf16[32,1,8,1024]{3,2,1,0:T(8,128)(2,1)S(1)}, u32[]{:S(2)}, u32[]{:S(2)}) async-start(bf16[32,1,8,1024]{3,2,1,0:T(8,128)(2,1)} %bitcast.8), calls=%async_computation.1 | async-start | bytes 1048576 | tf_op jit(solution)/shard_map/all_to_all | solution.py:146
  153.1 0.7 iota_compare_fusion.2
  153.9 0.6 fusion.46
  154.6 19.5 %all-to-all-done.1 = bf16[32,1,8,1024]{3,2,1,0:T(8,128)(2,1)S(1)} async-done(((bf16[32,1,8,1024]{3,2,1,0:T(8,128)(2,1)}), bf16[32,1,8,1024]{3,2,1,0:T(8,128)(2,1)S(1)}, u32[]{:S(2)}, u32[]{:S(2)}) %all-to-all-start.1) | async-done | bytes 524320 | tf_op jit(solution)/shard_map/all_to_all | solution.py:146
  174.1 0.6 gather_fusion
  174.8 1.8 dynamic_update_slice.5
  176.6 3.4 %broadcast_in_dim.61 = bf16[8,384,1024]{2,1,0:T(8,128)(2,1)} broadcast(bf16[384,1024]{1,0:T(8,128)(2,1)S(1)} %dynamic_update_slice.5), dimensions={1,2} | broadcast | bytes 7077888 | tf_op jit(solution)/shard_map/broadcast_in_dim | solution.py:19
  180.0 5.3 %all-to-all-start.2 = ((bf16[8,384,1024]{2,1,0:T(8,128)(2,1)}), bf16[8,384,1024]{2,1,0:T(8,128)(2,1)}, u32[]{:S(2)}, u32[]{:S(2)}) async-start(bf16[8,384,1024]{2,1,0:T(8,128)(2,1)} %broadcast_in_dim.61), calls=%async_computation.2 | async-start | bytes 12582912 | tf_op jit(solution)/shard_map/all_to_all | solution.py:18
  185.8 75.0 %all-gather.5.cloned.1.call-done = bf16[8192,768]{1,0:T(8,128)(2,1)} async-done(((bf16[256,768]{1,0:T(8,128)(2,1)}), bf16[8192,768]{1,0:T(8,128)(2,1)}) %all-gather.5.cloned.1.call-update) | async-done | bytes 12582928 | tf_op jit(solution)/shard_map/all_gather | solution.py:37
  260.8 7.1 %slice_bitcast_fusion = bf16[512,8192]{0,1:T(8,128)(2,1)} fusion(bf16[8192,768]{1,0:T(8,128)(2,1)} %all-gather.5.cloned.1.call-done), kind=kLoop, calls=%fused_computation.9 | loop fusion | bytes 16777216 | tf_op jit(solution)/shard_map/dot_general | solution.py:166
  267.9 11.9 %copy.58 = bf16[512,8192]{1,0:T(8,128)(2,1)} copy(bf16[512,8192]{0,1:T(8,128)(2,1)} %slice_bitcast_fusion) | data formatting | bytes 16777216 | tf_op jit(solution)/shard_map/dot_general | solution.py:166
  279.8 8.7 %copy.55 = bf16[8,384,1024]{1,2,0:T(8,128)(2,1)} copy(bf16[8,384,1024]{2,1,0:T(8,128)(2,1)} %all-to-all-done.2) | data formatting | bytes 12582912 | tf_op jit(solution)/shard_map/all_to_all | solution.py:18
  288.5 4.3 %fusion.2 = f32[384]{0:T(512)S(1)} fusion(bf16[8,384,1024]{1,2,0:T(8,128)(2,1)} %copy.55), kind=kLoop, calls=%fused_computation.6 | loop fusion | flops 9436800 | bytes 6292992 | tf_op jit(solution)/shard_map/reduce_sum | solution.py:159
  293.1 1.7 fusion.4
  294.9 4.8 %fusion.5 = f32[384,256]{0,1:S(1)} fusion(bf16[384,8192]{0,1:T(8,128)(2,1)S(1)} %bitcast.102, bf16[8192,768]{1,0:T(8,128)(2,1)} %all-gather.5.cloned.1.call-done), kind=kOutput, calls=%fused_computation.10 | convolution fusion | flops 1610612736 | bytes 10878976
  300.1 4.5 %fusion.56 = f32[384,4,128]{0,2,1:T(8,128)S(1)} fusion(bf16[384,8192,1]{0,1,2:T(8,128)(2,1)S(1)} %bitcast.103, bf16[4,128,8192]{2,1,0:T(8,128)(2,1)S(1)} %bitcast.101), kind=kOutput, calls=%fused_computation.102 | convolution fusion | flops 3221225472 | bytes 15466496 | tf_op jit(solution)/shard_map/dot_general | solution.py:166
  304.7 0.6 fusion.8
  305.9 0.9 convolution_convert_fusion
  306.8 0.9 copy.63
  (51 shorter events, 4.1 us)
Async XLA Ops:
  6.5 3.0 copy-start.2
  6.5 2.2 copy-start.1
  6.5 127.9 %all-gather.3.cloned.1.call-start = ((), (), s32[]{:S(2)}) async-start(), calls=%async_computation.3 | async-start | bytes 13516800 | tf_op jit(solution)/shard_map/all_gather | solution.py:139
  7.8 253.1 %all-gather.5.cloned.1.call-start = ((), (), s32[]{:S(2)}) async-start(), calls=%async_computation.4 | async-start | bytes 12976128 | tf_op jit(solution)/shard_map/all_gather | solution.py:37
  8.7 7.6 %copy-start.4 = (s32[32]{0:T(128)S(1)}, s32[32]{0:T(128)}, u32[]{:S(2)}) copy-start(s32[32]{0:T(128)} %param.18) | copy-start | bytes 388
  10.7 20.1 %all-to-all-start = ((bf16[8,8,8,2,400]{4,2,1,3,0:T(8,128)(2,1)}), bf16[8,8,8,2,400]{4,2,1,3,0:T(8,128)(2,1)S(1)}, u32[]{:S(2)}, u32[]{:S(2)}) async-start(bf16[8,8,8,2,400]{4,2,1,3,0:T(8,128)(2,1)} %broadcast_in_dim.55), calls=%async_computation | async-start | bytes 2097152 | tf_op jit(solution)/shard_map/all_to_all | solution.py:18
  33.7 100.7 %copy-start.5 = (f32[2,3200]{1,0:T(2,128)S(1)}, f32[2,3200]{1,0:T(2,128)}, u32[]{:S(2)}) copy-start(f32[2,3200]{1,0:T(2,128)} %param.12) | copy-start | bytes 76804
  33.7 100.7 %copy-start.6 = (f32[2,3200]{1,0:T(2,128)S(1)}, f32[2,3200]{1,0:T(2,128)}, u32[]{:S(2)}) copy-start(f32[2,3200]{1,0:T(2,128)} %param.11) | copy-start | bytes 76804
  146.8 27.2 %all-to-all-start.1 = ((bf16[32,1,8,1024]{3,2,1,0:T(8,128)(2,1)}), bf16[32,1,8,1024]{3,2,1,0:T(8,128)(2,1)S(1)}, u32[]{:S(2)}, u32[]{:S(2)}) async-start(bf16[32,1,8,1024]{3,2,1,0:T(8,128)(2,1)} %bitcast.8), calls=%async_computation.1 | async-start | bytes 1048576 | tf_op jit(solution)/shard_map/all_to_all | solution.py:146
  180.0 5.3 %copy-start.3 = (f32[8192]{0:T(1024)S(1)}, f32[8192]{0:T(1024)}, u32[]{:S(2)}) copy-start(f32[8192]{0:T(1024)} %param.15) | copy-start | bytes 98308
  180.0 99.9 %all-to-all-start.2 = ((bf16[8,384,1024]{2,1,0:T(8,128)(2,1)}), bf16[8,384,1024]{2,1,0:T(8,128)(2,1)}, u32[]{:S(2)}, u32[]{:S(2)}) async-start(bf16[8,384,1024]{2,1,0:T(8,128)(2,1)} %broadcast_in_dim.61), calls=%async_computation.2 | async-start | bytes 12582912 | tf_op jit(solution)/shard_map/all_to_all | solution.py:18
  288.5 4.6 %copy-start = (bf16[8,384,1024]{1,2,0:T(8,128)(2,1)S(1)}, bf16[8,384,1024]{1,2,0:T(8,128)(2,1)}, u32[]{:S(2)}) copy-start(bf16[8,384,1024]{1,2,0:T(8,128)(2,1)} %copy.55) | copy-start | bytes 18874372
  293.1 7.0 %slice-start = ((s8[8388608]{0:T(1024)(128)(4,1)}), s8[4194304]{0:T(1024)(128)(4,1)S(1)}, s32[]{:S(2)}) async-start(s8[8388608]{0:T(1024)(128)(4,1)} %bitcast.99), calls=%async_computation.5 | async-start | bytes 8388608
  294.8 5.2 %slice-start.1 = ((s8[8388608]{0:T(1024)(128)(4,1)}), s8[4194304]{0:T(1024)(128)(4,1)S(1)}, s32[]{:S(2)}) async-start(s8[8388608]{0:T(1024)(128)(4,1)} %bitcast.99), calls=%async_computation.6 | async-start | bytes 8388608
Sparse Core Ops, SparseCore 0:
  9.9 124.4 all-gather.2
  137.0 123.7 all-gather.4
where the time goes:
time: 316 us; the launch traced here: 315 us
  waiting for transfers between devices  206 us (65%)
  local copies, waits for them, and re-layouts  45.2 us (14%)
  matrix products  20.2 us (6%)
  starting transfers between devices  16.6 us (5%)
  between operations  14.3 us (5%)
  other arithmetic  12.2 us (4%)
    all_gather x1, waiting for transfers between devices, per_device(): lax.all_gather(proj_weight, 'dp', axis=0, tiled=True)  98.4 us
    all_gather x1, waiting for transfers between devices, sent_together(): lax.all_gather(both, axis, axis=dim, tiled=True)  75 us
    all_to_all x1, waiting for transfers between devices, per_device(): lax.all_to_all(empty_slots.at[owners, slots].set(image_cols), 'dp', split...  19.5 us
    dot_general x2, local copies, waits for them, and re-layouts, per_device(): jnp.dot(columns, weight_rows[0], preferred_element_type=jnp.float32)  19 us
    all_to_all x2, waiting for transfers between devices, from_everyone(): lax.all_to_all(jnp.broadcast_to(array[None], (count, *array.shape)), axis...  13.1 us
    all_to_all x2, starting transfers between devices, from_everyone(): lax.all_to_all(jnp.broadcast_to(array[None], (count, *array.shape)), axis...  10.9 us
    dot_general x1, matrix products, per_device(): jnp.einsum('rmf,fmo->ro', columns, lax.all_gather(proj_weight, 'dp', axis...  9.42 us
    all_to_all x1, local copies, waits for them, and re-layouts, from_everyone(): lax.all_to_all(jnp.broadcast_to(array[None], (count, *array.shape)), axis...  8.65 us
  transfers between devices with their start and end apart: 5, of which 4 were waited for; matrix products, arithmetic and copies ran while one was open for 15% of the time, Pallas kernels for 0%

commit v1 on v0

v1 whole, which is shorter than its diff:
```python
import functools

import jax
import jax.numpy as jnp
import numpy as np
from jax import lax
from jax.experimental import pallas as pl
from jax.experimental.pallas import tpu as pltpu
from jax.sharding import PartitionSpec as P

MESH = pl.DeviceIdType.MESH
BF = jnp.bfloat16
F32 = jnp.float32

HEAD_WIDTH = 128
SEQ = 384
TOK = 64
NX, NY, NZ = 4, 4, 8
LANES = 256
ROWS = 208
PART = 200
vision_epsilon = 1e-06
decoder_epsilon = 1e-05
rope_base = 500000.0

STARTS = (0, 0, 3, 5, 7)
SLOTS = max(STARTS) + 5


def dot(a, b):
    return jnp.dot(a, b, preferred_element_type=F32)


def lane_of(shape):
    return lax.broadcasted_iota(jnp.int32, shape, len(shape) - 1)


def row_of(shape):
    return lax.broadcasted_iota(jnp.int32, shape, len(shape) - 2)


def kernel(
    cnt_ref, off_ref, vis_ref, gain_ref, bias_ref, proj_ref, qkv_ref, text_ref, cos_ref, sin_ref,
    out_ref,
    wp, wq, vis_all, vis_own, stats, acts, vs, vr, im, ia, ot, rt, oi, ri, stt, rstt, sti, rsti,
    a2s, a2r,
    l_sem, z_s, z_r, st_s, st_r, b_s, b_r, d_s, d_r, vs_s, vs_r, t_s, t_r, i_s, i_r, n_s, n_r,
    a_s, a_r,
):
    dp = lax.axis_index("dp")
    tn = lax.axis_index("tensor")
    x, z = dp // NZ, dp % NZ
    y, c = tn // 2, tn % 2
    pending = []

    def remote(src, dst, ssem, rsem, to):
        return pltpu.make_async_remote_copy(
            src_ref=src, dst_ref=dst, send_sem=ssem, recv_sem=rsem, device_id=to,
            device_id_type=MESH,
        )

    def send(src, dst, ssem, rsem, to):
        copy = remote(src, dst, ssem, rsem, to)
        copy.start()
        pending.append(copy)

    here = (dp, tn)

    def arrived(ref, ssem, rsem):
        remote(ref, ref, ssem, rsem, here).wait_recv()

    def own(u):
        return proj_ref.at[u] if u < 2 else qkv_ref.at[u - 2]

    def slot_ref(u, source):
        if u < 2:
            return wp.at[u, source, pl.ds(0, ROWS)]
        return wq.at[u - 2, source]

    def goes(u, e, k):
        return k < 4 or (u % 2 == e)

    def ring(slot):
        for u, start in enumerate(STARTS):
            k = slot - start
            if k < 0 or k > 4:
                continue
            for e in range(2):
                sign = 1 if e == 0 else -1
                source = (z - sign * k + 2 * NZ) % NZ
                if k >= 1 and goes(u, e, k):
                    arrived(slot_ref(u, source), z_s.at[u, e, k - 1], z_r.at[u, e, k - 1])
                if k <= 3 and goes(u, e, k + 1):
                    to = (x * NZ + (z + sign + NZ) % NZ, tn)
                    src = own(u) if k == 0 else slot_ref(u, source)
                    send(src, slot_ref(u, source), z_s.at[u, e, k], z_r.at[u, e, k], to)

    def spread(kind, src, dst):
        for o in range(NY):
            to = (y * NZ + z, ((y + o) % NY) * 2 + c)
            copy = remote(src, dst, b_s.at[kind, o], b_r.at[kind, x], to)
            if o:
                copy.start()
                pending.append(copy)
            else:
                local = pltpu.make_async_copy(src, dst, b_r.at[kind, x])

                @pl.when(x != y)
                def _():
                    copy.start()

                @pl.when(x == y)
                def _():
                    local.start()

    def spread_done(kind, src, dst):
        copy = remote(src, dst, b_s.at[kind, 0], b_r.at[kind, x], (y * NZ + z, y * 2 + c))

        @pl.when(x != y)
        def _():
            copy.wait_send()

    def to_sibling(kind, place):
        for s in range(NX):
            arrived(place(c, s), b_s.at[kind, 0], b_r.at[kind, s])
            send(place(c, s), place(c, s), d_s.at[kind, s], d_r.at[kind, s], (dp, tn + 1 - 2 * c))

    def from_sibling(kind, place):
        for s in range(NX):
            arrived(place(1 - c, s), d_s.at[kind, s], d_r.at[kind, s])

    def vis_place(core, s):
        return vis_all.at[pl.ds(4 * core, 4), s]

    def text_place(core, s):
        return acts.at[core, s]

    def image_place(core, s):
        return ia.at[core, s]

    def along_x(o):
        return (((x + o) % NX) * NZ + z, tn)

    ring(0)
    locals_ = []
    for u in range(5):
        local = pltpu.make_async_copy(own(u), slot_ref(u, z), l_sem.at[u])
        local.start()
        locals_.append(local)

    xv = vis_ref[...].astype(F32)
    mean = jnp.sum(jnp.sum(xv, axis=0), axis=-1, keepdims=True) / (4 * PART)
    centred = jnp.where(lane_of(xv.shape) < PART, xv - mean[None], 0.0)
    m2 = jnp.sum(jnp.sum(centred * centred, axis=0), axis=-1, keepdims=True)
    stats[tn] = jnp.where(lane_of((TOK, 128)) == 0, mean, m2)
    for o in range(1, 8):
        send(stats.at[tn], stats.at[tn], st_s.at[o - 1], st_r.at[o - 1], (dp, (tn + o) % 8))
    for u in range(2):
        for s in range(NZ):
            wp[u, s, ROWS:LANES, :] = jnp.zeros((LANES - ROWS, 512), BF)
    for o in range(1, 8):
        arrived(stats.at[(tn - o + 8) % 8], st_s.at[o - 1], st_r.at[o - 1])
    means = [stats[t][:, 0:1] for t in range(8)]
    mean = sum(means[1:], means[0]) / 8.0
    total = jnp.zeros((TOK, 1), F32)
    for t in range(8):
        apart = means[t] - mean
        total = total + stats[t][:, 1:2] + (4.0 * PART) * apart * apart
    scale = lax.rsqrt(total / (32.0 * PART) + vision_epsilon)
    for i in range(4):
        piece = vis_ref[i].astype(F32)
        vis_own[i] = ((piece - mean) * scale * gain_ref[i] + bias_ref[i]).astype(BF)
    spread(0, vis_own, vis_place(c, x))
    spread(1, text_ref, text_place(c, x))

    def vision():
        from_sibling(0, vis_place)
        for h in range(2):
            acc = None
            for s in range(NZ):
                term = dot(vis_all[s].reshape(NX * TOK, LANES), wp[h, s])
                acc = term if acc is None else acc + term
            cols = pl.ds(512 * h, 512)
            vs[:, :, cols] = acc.reshape(NX, TOK, 512).astype(BF)
        for o in range(1, NX):
            send(vs.at[(x + o) % NX], vr.at[o - 1], vs_s.at[o - 1], vs_r.at[o - 1], along_x(o))

    def image():
        acc = vs[x].astype(F32)
        for o in range(1, NX):
            arrived(vr.at[o - 1], vs_s.at[o - 1], vs_r.at[o - 1])
            acc = acc + vr[o - 1].astype(F32)
        im[...] = acc.astype(BF)
        spread(2, im, image_place(c, x))

    def squares(source, o, rows):
        s = (x + o) % NX
        acc = jnp.zeros((rows, 1), F32)
        for core in range(2):
            v = source[core, s].astype(F32)
            acc = acc + jnp.sum(v * v, axis=-1, keepdims=True)
        high = acc.astype(BF).astype(F32)
        mid = (acc - high).astype(BF).astype(F32)
        low = acc - high - mid
        lane = lane_of((rows, 128))
        return jnp.where(lane == 0, high, jnp.where(lane == 1, mid, low)).astype(BF)

    def text_squares():
        for o in range(NX):
            if o == 0:
                rstt[0] = squares(acts, 0, SEQ)
            else:
                stt[o - 1] = squares(acts, o, SEQ)
        for o in range(1, NX):
            send(stt.at[o - 1], rstt.at[o], n_s.at[0, o - 1], n_r.at[0, o - 1], along_x(o))

    def image_squares():
        for o in range(NX):
            if o == 0:
                rsti[0] = squares(ia, 0, TOK)
            else:
                sti[o - 1] = squares(ia, o, TOK)
        for o in range(1, NX):
            send(sti.at[o - 1], rsti.at[o], n_s.at[1, o - 1], n_r.at[1, o - 1], along_x(o))

    def project(source, u, o):
        s = (x + o) % NX
        first = dot(source[0, s], wq[u, 0:4].reshape(1024, 256))
        return first + dot(source[1, s], wq[u, 4:8].reshape(1024, 256))

    def text_unit(u):
        for o in (2, 1, 3, 0):
            value = project(acts, u, o).astype(BF)
            if o == 0:
                rt[u, 0] = value
            else:
                ot[u, o - 1] = value
                send(ot.at[u, o - 1], rt.at[u, o], t_s.at[u, o - 1], t_r.at[u, o - 1], along_x(o))

    def image_unit(u):
        for o in (2, 1, 3, 0):
            value = project(ia, u, o).astype(BF)
            if o == 0:
                ri[u, 0] = value
            else:
                oi[u, o - 1] = value
                send(oi.at[u, o - 1], ri.at[u, o], i_s.at[u, o - 1], i_r.at[u, o - 1], along_x(o))

    def locals_done(us):
        for u in us:
            locals_[u].wait()

    for slot in range(1, SLOTS):
        ring(slot)
        if slot == 1:
            to_sibling(0, vis_place)
        if slot == 4:
            locals_done((0, 1))
            vision()
        if slot == 5:
            to_sibling(1, text_place)
        if slot == 6:
            image()
            from_sibling(1, text_place)
            text_squares()
        if slot == 7:
            locals_done((2, 3, 4))
            text_unit(0)
        if slot == 8:
            to_sibling(2, image_place)
        if slot == 9:
            from_sibling(2, image_place)
            text_unit(1)
            image_squares()
            image_unit(0)
            image_unit(1)
        if slot == 11:
            image_unit(2)

    first = jnp.int32(0)
    my_first = jnp.int32(0)
    my_count = jnp.int32(0)
    owners = [jnp.int32(0)] * 8
    for s in range(NX * NZ):
        count = cnt_ref[s]
        my_first = my_first + jnp.where(s < dp, count, 0)
        my_count = my_count + jnp.where(s == dp, count, 0)
        first = first + count
        owners = [a + jnp.where(first <= r * 32 + dp, 1, 0) for r, a in enumerate(owners)]
    shape = (512, 128)
    row, col = row_of(shape), lane_of(shape)
    owner = jnp.zeros(shape, jnp.int32)
    for r in range(8):
        owner = jnp.where(((col >> 3) & 7) == r, owners[r], owner)
    same = ((row >> 4) == owner) & (((row >> 3) & 1) == (col >> 6)) & ((row & 7) == (col & 7))
    pick = jnp.where(same, 1.0, 0.0).astype(BF)

    def gathered(buffer, rows, sems, receives):
        acc = buffer[0].astype(F32)
        for o in range(1, NX):
            arrived(buffer.at[o], sems.at[o - 1], receives.at[o - 1])
            acc = acc + buffer[o].astype(F32)
        return acc

    def row_scale(buffer, rows, which):
        acc = gathered(buffer, rows, n_s.at[which], n_r.at[which])
        total = jnp.sum(jnp.where(lane_of(acc.shape) < 3, acc, 0.0), axis=-1, keepdims=True)
        return lax.rsqrt(total / 8192.0 + decoder_epsilon)

    image_scale = row_scale(rsti, TOK, 1)
    pieces = [(gathered(ri.at[u], TOK, i_s.at[u], i_r.at[u]) * image_scale).astype(BF)
              for u in range(3)]
    low = jnp.concatenate([pieces[0], pieces[1][:, 0:128]], axis=1)
    high = jnp.concatenate([pieces[1][:, 128:256], pieces[2]], axis=1)
    both = jnp.concatenate([low, high], axis=0)
    a2s[...] = dot(pick, both).astype(BF).reshape(32, 16, 384)
    a2r[dp] = a2s[dp]

    def route(o, carry):
        to = (dp + o) % 32
        remote(a2s.at[to], a2r.at[dp], a_s.at[o - 1], a_r.at[o - 1], (to, tn)).start()
        return carry

    lax.fori_loop(1, 32, route, 0)
    text_unit(2)

    shape = (SEQ, 512)
    row, col = row_of(shape), lane_of(shape)
    place = row - off_ref[0]
    inside = (place >= 0) & (place < 8 * my_count)
    source = (my_first + (place >> 3)) & 31
    match = inside & ((col >> 4) == source) & ((col & 7) == (place & 7))
    sel_low = jnp.where(match & (((col >> 3) & 1) == 0), 1.0, 0.0).astype(BF)
    sel_high = jnp.where(match & (((col >> 3) & 1) == 1), 1.0, 0.0).astype(BF)
    place = row_of((SEQ, 128)) - off_ref[0]
    is_image = (place >= 0) & (place < 8 * my_count)
    causal = row_of((SEQ, SEQ)) >= lane_of((SEQ, SEQ))
    text_scale = row_scale(rstt, SEQ, 0)

    def route_done(o, carry):
        source = (dp - o + 32) % 32
        remote(a2s.at[source], a2r.at[source], a_s.at[o - 1], a_r.at[o - 1], here).wait_recv()
        return carry

    lax.fori_loop(1, 32, route_done, 0)
    routed = a2r[...].reshape(512, 384)
    image_low = dot(sel_low, routed)
    image_high = dot(sel_high, routed)

    texts = [gathered(rt.at[u], SEQ, t_s.at[u], t_r.at[u]) * text_scale for u in range(3)]
    cos, sin = cos_ref[...], sin_ref[...]

    def column(i):
        text = texts[i // 2][:, 128 * (i % 2) : 128 * (i % 2) + 128]
        picture = image_low if i < 3 else image_high
        picture = picture[:, 128 * (i % 3) : 128 * (i % 3) + 128]
        return jnp.where(is_image, picture, text)

    def turned(value):
        return (value * cos + pltpu.roll(value, 64, 1) * sin).astype(BF)

    key = turned(column(4))
    value = column(5).astype(BF)
    for h in range(4):
        query = turned(column(h))
        scores = lax.dot_general(query, key, (((1,), (1,)), ((), ())), preferred_element_type=F32)
        scores = jnp.where(causal, scores * HEAD_WIDTH ** (-0.5), -1e30)
        powers = jnp.exp(scores - jnp.max(scores, axis=-1, keepdims=True))
        weights = (powers / jnp.sum(powers, axis=-1, keepdims=True)).astype(BF)
        out_ref[:, 128 * h : 128 * h + 128] = dot(weights, value).astype(BF)

    for copy in pending:
        copy.wait_send()
    spread_done(0, vis_own, vis_place(c, x))
    spread_done(1, text_ref, text_place(c, x))
    spread_done(2, im, image_place(c, x))

    def sent(o, carry):
        to = (dp + o) % 32
        remote(a2s.at[to], a2r.at[dp], a_s.at[o - 1], a_r.at[o - 1], here).wait_send()
        return carry

    lax.fori_loop(1, 32, sent, 0)


def rotation_tables():
    exponents = np.arange(64, dtype=np.float32) * np.float32(2.0 / 128)
    frequency = np.float32(rope_base) ** (-exponents)
    angles = np.arange(SEQ, dtype=np.float32)[:, None] * frequency[None, :]
    cos, sin = np.cos(angles), np.sin(angles)
    return (
        np.concatenate([cos, cos], axis=1).astype(np.float32),
        np.concatenate([-sin, sin], axis=1).astype(np.float32),
    )


def per_device(vis_rows, ln_gain, ln_bias, proj_weight, text_rows, attn_gain, w_query,
               key_value_weight, tile_counts, image_offsets):
    dp = lax.axis_index("dp")
    tn = lax.axis_index("tensor")

    def lanes(a):
        return jnp.pad(a, [(0, 0)] * (a.ndim - 1) + [(0, LANES - PART)])

    vis = vis_rows.reshape(TOK, 2, 4, 100).transpose(2, 0, 3, 1).reshape(4, TOK, PART)
    vis = lanes(vis)

    def features(a):
        a = lax.dynamic_slice_in_dim(a, tn * 400, 400, 1)
        return lanes(a.reshape(2, 4, 100).transpose(1, 2, 0).reshape(4, 1, PART))

    proj = jnp.pad(proj_weight.reshape(PART, 1024), ((0, ROWS - PART), (0, 0)))
    proj = proj.reshape(ROWS, 2, 512).transpose(1, 0, 2)
    rows = lax.dynamic_slice_in_dim(attn_gain, dp * 256, 256, 0)[:, None]
    qkv = jnp.concatenate([w_query, key_value_weight.reshape(256, 256)], axis=1)
    qkv = (qkv.astype(F32) * rows).astype(BF).reshape(256, 3, 256).transpose(1, 0, 2)
    cos, sin = rotation_tables()
    vmem = pl.BlockSpec(memory_space=pltpu.VMEM)
    smem = pl.BlockSpec(memory_space=pltpu.SMEM)
    dma = pltpu.SemaphoreType.DMA
    out = pl.pallas_call(
        kernel,
        out_shape=jax.ShapeDtypeStruct((SEQ, 512), BF),
        in_specs=[smem, smem] + [vmem] * 8,
        out_specs=vmem,
        scratch_shapes=[
            pltpu.VMEM((2, NZ, LANES, 512), BF),
            pltpu.VMEM((3, NZ, 256, 256), BF),
            pltpu.VMEM((NZ, NX, TOK, LANES), BF),
            pltpu.VMEM((4, TOK, LANES), BF),
            pltpu.VMEM((8, TOK, 128), F32),
            pltpu.VMEM((2, NX, SEQ, 1024), BF),
            pltpu.VMEM((NX, TOK, 1024), BF),
            pltpu.VMEM((NX - 1, TOK, 1024), BF),
            pltpu.VMEM((TOK, 1024), BF),
            pltpu.VMEM((2, NX, TOK, 1024), BF),
            pltpu.VMEM((3, NX - 1, SEQ, 256), BF),
            pltpu.VMEM((3, NX, SEQ, 256), BF),
            pltpu.VMEM((3, NX - 1, TOK, 256), BF),
            pltpu.VMEM((3, NX, TOK, 256), BF),
            pltpu.VMEM((NX - 1, SEQ, 128), BF),
            pltpu.VMEM((NX, SEQ, 128), BF),
            pltpu.VMEM((NX - 1, TOK, 128), BF),
            pltpu.VMEM((NX, TOK, 128), BF),
            pltpu.VMEM((32, 16, 384), BF),
            pltpu.VMEM((32, 16, 384), BF),
            dma((5,)),
            dma((5, 2, 4)),
            dma((5, 2, 4)),
            dma((7,)),
            dma((7,)),
            dma((3, NY)),
            dma((3, NX)),
            dma((3, NX)),
            dma((3, NX)),
            dma((3,)),
            dma((3,)),
            dma((3, 3)),
            dma((3, 3)),
            dma((3, 3)),
            dma((3, 3)),
            dma((2, 3)),
            dma((2, 3)),
            dma((31,)),
            dma((31,)),
        ],
        compiler_params=pltpu.CompilerParams(has_side_effects=True, vmem_limit_bytes=60 << 20),
        name="step",
    )(tile_counts, image_offsets, vis, features(ln_gain), features(ln_bias), proj, qkv,
      text_rows[0], jnp.asarray(cos), jnp.asarray(sin))
    return out[None]


def solution(mesh):
    in_specs = (
        P(None, "dp", None, "tensor"),
        P(),
        P(),
        P("dp", None, "tensor"),
        P("dp", None, "tensor"),
        P(),
        P("dp", "tensor"),
        P("dp", None, "tensor"),
        P(),
        P("dp"),
    )
    return jax.shard_map(per_device, mesh=mesh, in_specs=in_specs,
                         out_specs=P("dp", None, "tensor"), check_vma=False)
```

time: 316 us -> 295 us (0.934)
  Pallas kernels: 0 us -> 283 us
  waiting for transfers between devices: 206 us -> 0 us
  local copies, waits for them, and re-layouts: 45.2 us -> 8.77 us
  matrix products: 20.2 us -> 0 us
  starting transfers between devices: 16.6 us -> 0 us
  between operations: 14.3 us -> 0.75 us
  other arithmetic: 12.2 us -> 0.89 us
    pallas_call x0 -> x1, Pallas kernels: none -> 283 us  [per_device(): pl.pallas_call(kernel, out_shape=jax.ShapeDtypeStruct((SEQ, 512), BF), in...]
    all_gather x2 -> x0, waiting for transfers between devices: 173 us -> none  [the longest x1 98.4 us: per_device(): lax.all_gather(proj_weight, 'dp', axis=0, tiled=True)]
    all_to_all x3 -> x0, waiting for transfers between devices: 32.6 us -> none  [the longest x1 19.5 us: per_device(): lax.all_to_all(empty_slots.at[owners, slots].set(image_cols), 'dp', split...]
    dot_general x2 -> x0, local copies, waits for them, and re-layouts: 19 us -> none  [per_device(): jnp.dot(columns, weight_rows[0], preferred_element_type=jnp.float32)]
    all_to_all x3 -> x0, starting transfers between devices: 16.5 us -> none  [the longest x2 10.9 us: from_everyone(): lax.all_to_all(jnp.broadcast_to(array[None], (count, *array.shape)), axis...]
    dot_general x4 -> x0, matrix products: 15.4 us -> none  [the longest x1 9.42 us: per_device(): jnp.einsum('rmf,fmo->ro', columns, lax.all_gather(proj_weight, 'dp', axis...]
    all_to_all x1 -> x0, local copies, waits for them, and re-layouts: 8.65 us -> none  [from_everyone(): lax.all_to_all(jnp.broadcast_to(array[None], (count, *array.shape)), axis...]
    reduce_sum x7 -> x0, other arithmetic: 6.67 us -> none  [the longest x1 4.35 us: per_device(): mean_square = jnp.mean(seq_float * seq_float, axis=-1, keepdims=True)]
  transfers between devices with their start and end apart: 5 -> 0, of which waited for: 4 -> 0; matrix products, arithmetic and copies ran while one was open for 15% -> 0% of each run, Pallas kernels for 0% -> 0%
where the time goes in v1:
time: 295 us; the launch traced here: 293 us
  Pallas kernels  283 us (96%)
  local copies, waits for them, and re-layouts  8.77 us (3%)
    pallas_call x1, Pallas kernels, per_device(): pl.pallas_call(kernel, out_shape=jax.ShapeDtypeStruct((SEQ, 512), BF), in...  283 us

profile of v1, /device:TPU:8, one launch (start us, length us, event | category | flops | bytes accessed | tf_op | source)
XLA Modules:
  0.0 293.4 jit_solution(8897883624037159593)
XLA Ops:
  0.0 0.0 copy-start.1
  0.0 0.8 constant_dynamic-slice_fusion
  0.8 0.1 reshape.39
  0.9 0.2 copy.16
  1.1 0.1 copy.17
  1.1 0.6 pad.16.gain_ref
  1.8 0.1 reshape.41
  1.8 0.1 copy.18
  2.0 0.1 copy.19
  2.1 0.6 pad.17.bias_ref
  2.7 0.8 dynamic_slice.11
  3.4 0.0 copy-done.1
  3.5 0.0 copy-start.2
  3.5 0.1 copy.22
  3.6 0.8 copy-done.2
  4.4 0.1 copy.21
  4.5 0.2 copy.23
  4.7 0.0 copy-start
  4.7 0.9 fusion.qkv_ref
  5.6 0.1 copy-done
  5.7 0.2 reshape.43
  5.9 0.0 copy-start.3
  5.9 0.8 copy.26
  6.7 0.1 copy-done.3
  6.8 0.1 reshape.37
  7.0 0.2 copy.14
  7.2 0.1 copy.15
  7.3 0.7 pad.15.vis_ref
  8.6 283.0 %step.1 = bf16[384,512]{1,0:T(8,128)(2,1)} custom-call(s32[32]{0:T(128)} %cnt_ref.1, s32[1]{0:T(128)S(6)} %copy.28.off_ref, bf16[4,64,256]{2,1,0:T(8,128)(2,1)} %pad.15.vis_ref, f32[4,1,256]{2,1,0:T(1,128)} %pad.16.gain_ref, f32[4,1,256]{2,1,0:T(1,128)} %pad.17.bias_ref, bf16[2,208,512]{2,1,0:T(8,128)(2,1)} %bitcast.21, bf16[3,256,256]{2,1,0:T(8,128)(2,1)} %fusion.qkv_ref, ...), custom_call_target="tpu_custom_call" | custom-call | tf_op jit(solution)/shard_map/step/pallas_call | solution.py:421
  291.6 1.8 copy.29
  (2 shorter events, 0.1 us)
Async XLA Ops:
  0.0 3.5 %copy-start.1 = (bf16[256,512]{1,0:T(8,128)(2,1)S(1)}, bf16[256,512]{1,0:T(8,128)(2,1)}, u32[]{:S(2)}) copy-start(bf16[256,512]{1,0:T(8,128)(2,1)} %param.18) | copy-start | bytes 786436
  3.5 0.9 copy-start.2
  4.7 1.0 copy-start
  5.9 0.9 copy-start.3

commit v2 on v1

--- a/solution.py
+++ b/solution.py
@@ -43,8 +43,8 @@
     cnt_ref, off_ref, vis_ref, gain_ref, bias_ref, proj_ref, qkv_ref, text_ref, cos_ref, sin_ref,
     out_ref,
     wp, wq, vis_all, vis_own, stats, acts, vs, vr, im, ia, ot, rt, oi, ri, stt, rstt, sti, rsti,
-    a2s, a2r,
-    l_sem, z_s, z_r, st_s, st_r, b_s, b_r, d_s, d_r, vs_s, vs_r, t_s, t_r, i_s, i_r, n_s, n_r,
+    a2s, a2r, vis_col, text_col, im_col,
+    l_sem, z_s, z_r, st_s, st_r, ys_s, ys_r, xs_s, xs_r, d_s, d_r, vs_s, vs_r, t_s, t_r, i_s, i_r, n_s, n_r,
     a_s, a_r,
 ):
     dp = lax.axis_index("dp")
@@ -95,48 +95,87 @@
                     src = own(u) if k == 0 else slot_ref(u, source)
                     send(src, slot_ref(u, source), z_s.at[u, e, k], z_r.at[u, e, k], to)
 
-    def spread(kind, src, dst):
-        for o in range(NY):
-            to = (y * NZ + z, ((y + o) % NY) * 2 + c)
-            copy = remote(src, dst, b_s.at[kind, o], b_r.at[kind, x], to)
-            if o:
+    class Spread:
+        def __init__(self, kind, own, column, place):
+            self.kind, self.own, self.column, self.place = kind, own, column, place
+
+        def on_y(self, src, slot, h, step):
+            k = self.kind
+            send(src, self.column(slot, h), ys_s.at[k, slot, h], ys_r.at[k, slot, h],
+                 (dp, ((y + step + NY) % NY) * 2 + c))
+
+        def on_x(self, src, j, h, kappa):
+            k = self.kind
+            copy = remote(src, self.place(c, x, h), xs_s.at[k, j, h], xs_r.at[k, x, h],
+                          (kappa * NZ + z, tn))
+            local = pltpu.make_async_copy(src, self.place(c, x, h), xs_r.at[k, x, h])
+
+            @pl.when(kappa != x)
+            def _():
                 copy.start()
-                pending.append(copy)
-            else:
-                local = pltpu.make_async_copy(src, dst, b_r.at[kind, x])
-
-                @pl.when(x != y)
-                def _():
-                    copy.start()
-
-                @pl.when(x == y)
-                def _():
-                    local.start()
-
-    def spread_done(kind, src, dst):
-        copy = remote(src, dst, b_s.at[kind, 0], b_r.at[kind, x], (y * NZ + z, y * 2 + c))
-
-        @pl.when(x != y)
-        def _():
-            copy.wait_send()
-
-    def to_sibling(kind, place):
-        for s in range(NX):
-            arrived(place(c, s), b_s.at[kind, 0], b_r.at[kind, s])
-            send(place(c, s), place(c, s), d_s.at[kind, s], d_r.at[kind, s], (dp, tn + 1 - 2 * c))
-
-    def from_sibling(kind, place):
-        for s in range(NX):
-            arrived(place(1 - c, s), d_s.at[kind, s], d_r.at[kind, s])
-
-    def vis_place(core, s):
-        return vis_all.at[pl.ds(4 * core, 4), s]
-
-    def text_place(core, s):
-        return acts.at[core, s]
-
-    def image_place(core, s):
-        return ia.at[core, s]
+
+            @pl.when(kappa == x)
+            def _():
+                local.start()
+
+            later.append((copy, kappa))
+
+        def begin(self):
+            for h in range(2):
+                self.on_y(self.own(h), 0, h, 1)
+                self.on_y(self.own(h), 1, h, -1)
+            for h in range(2):
+                self.on_x(self.own(h), 3, h, y)
+
+        def near(self, h):
+            k = self.kind
+            for slot, step in ((0, 1), (1, -1)):
+                arrived(self.column(slot, h), ys_s.at[k, slot, h], ys_r.at[k, slot, h])
+                if slot == h:
+                    src = self.column(slot, h)
+                    send(src, self.column(2, h), ys_s.at[k, 2, h], ys_r.at[k, 2, h],
+                         (dp, ((y + step + NY) % NY) * 2 + c))
+            for slot, step in ((0, 1), (1, -1)):
+                self.on_x(self.column(slot, h), slot, h, (y - step + NY) % NY)
+
+        def far(self, h):
+            k = self.kind
+            arrived(self.column(2, h), ys_s.at[k, 2, h], ys_r.at[k, 2, h])
+            self.on_x(self.column(2, h), 2, h, (y + 2) % NY)
+
+        def to_sibling(self):
+            k = self.kind
+            for s in range(NX):
+                for h in range(2):
+                    ref = self.place(c, s, h)
+                    arrived(ref, xs_s.at[k, 0, h], xs_r.at[k, s, h])
+                    send(ref, ref, d_s.at[k, s, h], d_r.at[k, s, h], (dp, tn + 1 - 2 * c))
+
+        def from_sibling(self):
+            k = self.kind
+            for s in range(NX):
+                for h in range(2):
+                    arrived(self.place(1 - c, s, h), d_s.at[k, s, h], d_r.at[k, s, h])
+
+    later = []
+    vis_spread = Spread(
+        0,
+        lambda h: vis_own.at[pl.ds(2 * h, 2)],
+        lambda j, h: vis_col.at[j, pl.ds(2 * h, 2)],
+        lambda core, s, h: vis_all.at[pl.ds(4 * core + 2 * h, 2), s],
+    )
+    text_spread = Spread(
+        1,
+        lambda h: text_ref.at[pl.ds(192 * h, 192)],
+        lambda j, h: text_col.at[j, pl.ds(192 * h, 192)],
+        lambda core, s, h: acts.at[core, s, pl.ds(192 * h, 192)],
+    )
+    image_spread = Spread(
+        2,
+        lambda h: im.at[pl.ds(32 * h, 32)],
+        lambda j, h: im_col.at[j, pl.ds(32 * h, 32)],
+        lambda core, s, h: ia.at[core, s, pl.ds(32 * h, 32)],
+    )
 
     def along_x(o):
         return (((x + o) % NX) * NZ + z, tn)
@@ -170,11 +209,11 @@
     for i in range(4):
         piece = vis_ref[i].astype(F32)
         vis_own[i] = ((piece - mean) * scale * gain_ref[i] + bias_ref[i]).astype(BF)
-    spread(0, vis_own, vis_place(c, x))
-    spread(1, text_ref, text_place(c, x))
+    vis_spread.begin()
+    text_spread.begin()
 
     def vision():
-        from_sibling(0, vis_place)
+        vis_spread.from_sibling()
         for h in range(2):
             acc = None
             for s in range(NZ):
@@ -191,7 +230,7 @@
             arrived(vr.at[o - 1], vs_s.at[o - 1], vs_r.at[o - 1])
             acc = acc + vr[o - 1].astype(F32)
         im[...] = acc.astype(BF)
-        spread(2, im, image_place(c, x))
+        image_spread.begin()
 
     def squares(source, o, rows):
         s = (x + o) % NX
@@ -253,23 +292,36 @@
     for slot in range(1, SLOTS):
         ring(slot)
         if slot == 1:
-            to_sibling(0, vis_place)
+            vis_spread.near(0)
+            vis_spread.near(1)
+            text_spread.near(0)
+            vis_spread.far(0)
+            vis_spread.far(1)
+        if slot == 2:
+            vis_spread.to_sibling()
+            text_spread.near(1)
+        if slot == 3:
+            text_spread.far(0)
+            text_spread.far(1)
         if slot == 4:
             locals_done((0, 1))
             vision()
         if slot == 5:
-            to_sibling(1, text_place)
+            text_spread.to_sibling()
         if slot == 6:
             image()
-            from_sibling(1, text_place)
+            text_spread.from_sibling()
+            image_spread.near(0)
+            image_spread.near(1)
             text_squares()
+            image_spread.far(0)
+            image_spread.far(1)
         if slot == 7:
             locals_done((2, 3, 4))
             text_unit(0)
-        if slot == 8:
-            to_sibling(2, image_place)
+            image_spread.to_sibling()
         if slot == 9:
-            from_sibling(2, image_place)
+            image_spread.from_sibling()
             text_unit(1)
             image_squares()
             image_unit(0)
@@ -371,9 +423,12 @@
 
     for copy in pending:
         copy.wait_send()
-    spread_done(0, vis_own, vis_place(c, x))
-    spread_done(1, text_ref, text_place(c, x))
-    spread_done(2, im, image_place(c, x))
+    for copy, kappa in later:
+
+        @pl.when(kappa != x)
+        def _(copy=copy):
+            copy.wait_send()
+
 
     def sent(o, carry):
         to = (dp + o) % 32
@@ -444,15 +499,20 @@
             pltpu.VMEM((NX, TOK, 128), BF),
             pltpu.VMEM((32, 16, 384), BF),
             pltpu.VMEM((32, 16, 384), BF),
+            pltpu.VMEM((3, 4, TOK, LANES), BF),
+            pltpu.VMEM((3, SEQ, 1024), BF),
+            pltpu.VMEM((3, TOK, 1024), BF),
             dma((5,)),
             dma((5, 2, 4)),
             dma((5, 2, 4)),
             dma((7,)),
             dma((7,)),
-            dma((3, NY)),
-            dma((3, NX)),
-            dma((3, NX)),
-            dma((3, NX)),
+            dma((3, 3, 2)),
+            dma((3, 3, 2)),
+            dma((3, 4, 2)),
+            dma((3, NX, 2)),
+            dma((3, NX, 2)),
+            dma((3, NX, 2)),
             dma((3,)),
             dma((3,)),
             dma((3, 3)),

time: 295 us -> 180 us (0.61)
  Pallas kernels: 283 us -> 169 us
    pallas_call x1, Pallas kernels: 283 us -> 169 us  [per_device(): pl.pallas_call(kernel, out_shape=jax.ShapeDtypeStruct((SEQ, 512), BF), in...]
where the time goes in v2:
time: 180 us
  Pallas kernels  169 us (94%)
  local copies, waits for them, and re-layouts  8.77 us (5%)
    pallas_call x1, Pallas kernels, per_device(): pl.pallas_call(kernel, out_shape=jax.ShapeDtypeStruct((SEQ, 512), BF), in...  169 us

profile of v2, /device:TPU:8, one launch (start us, length us, event | category | flops | bytes accessed | tf_op | source)
XLA Modules:
  0.0 179.7 jit_solution(17298141133126533492)
XLA Ops:
  0.0 0.0 copy-start.1
  0.0 0.8 constant_dynamic-slice_fusion
  0.8 0.1 reshape.39
  0.9 0.2 copy.16
  1.1 0.1 copy.17
  1.1 0.6 pad.16.gain_ref
  1.8 0.1 reshape.41
  1.8 0.1 copy.18
  2.0 0.1 copy.19
  2.1 0.6 pad.17.bias_ref
  2.7 0.8 dynamic_slice.11
  3.4 0.0 copy-done.1
  3.5 0.0 copy-start.2
  3.5 0.1 copy.22
  3.6 0.8 copy-done.2
  4.4 0.1 copy.21
  4.5 0.2 copy.23
  4.7 0.0 copy-start
  4.7 0.9 fusion.qkv_ref
  5.6 0.1 copy-done
  5.7 0.2 reshape.43
  5.9 0.0 copy-start.3
  5.9 0.8 copy.26
  6.7 0.1 copy-done.3
  6.8 0.1 reshape.37
  7.0 0.2 copy.14
  7.2 0.1 copy.15
  7.3 0.7 pad.15.vis_ref
  8.6 169.3 %step.1 = bf16[384,512]{1,0:T(8,128)(2,1)} custom-call(s32[32]{0:T(128)} %cnt_ref.1, s32[1]{0:T(128)S(6)} %copy.28.off_ref, bf16[4,64,256]{2,1,0:T(8,128)(2,1)} %pad.15.vis_ref, f32[4,1,256]{2,1,0:T(1,128)} %pad.16.gain_ref, f32[4,1,256]{2,1,0:T(1,128)} %pad.17.bias_ref, bf16[2,208,512]{2,1,0:T(8,128)(2,1)} %bitcast.21, bf16[3,256,256]{2,1,0:T(8,128)(2,1)} %fusion.qkv_ref, ...), custom_call_target="tpu_custom_call" | custom-call | tf_op jit(solution)/shard_map/step/pallas_call | solution.py:476
  177.9 1.8 copy.29
  (2 shorter events, 0.1 us)
Async XLA Ops:
  0.0 3.5 %copy-start.1 = (bf16[256,512]{1,0:T(8,128)(2,1)S(1)}, bf16[256,512]{1,0:T(8,128)(2,1)}, u32[]{:S(2)}) copy-start(bf16[256,512]{1,0:T(8,128)(2,1)} %param.18) | copy-start | bytes 786436
  3.5 0.9 copy-start.2
  4.7 1.0 copy-start
  5.9 0.9 copy-start.3

commit v3 on v2

--- a/solution.py
+++ b/solution.py
@@ -23,7 +23,7 @@
 decoder_epsilon = 1e-05
 rope_base = 500000.0
 
-STARTS = (0, 0, 3, 5, 7)
+STARTS = (0, 0, 3, 4, 5)
 SLOTS = max(STARTS) + 5
 
 
@@ -42,9 +42,10 @@
 def kernel(
     cnt_ref, off_ref, vis_ref, gain_ref, bias_ref, proj_ref, qkv_ref, text_ref, cos_ref, sin_ref,
     out_ref,
-    wp, wq, vis_all, vis_own, stats, acts, vs, vr, im, ia, ot, rt, oi, ri, stt, rstt, sti, rsti,
-    a2s, a2r, vis_col, text_col, im_col,
-    l_sem, z_s, z_r, st_s, st_r, ys_s, ys_r, xs_s, xs_r, d_s, d_r, vs_s, vs_r, t_s, t_r, i_s, i_r, n_s, n_r,
+    wp, wq, vis_all, vis_own, stats, acts, vs, im, ia, n_out, n_in,
+    v_fo, v_fi, v_no, v_ni, v_own, i_fo, i_fi, i_no, i_ni, i_own, t_fo, t_fi, t_no, t_ni, t_own,
+    a2s, a2r, vis_col, text_col, im_col, text_relay,
+    l_sem, z_s, z_r, st_s, st_r, ys_s, ys_r, xs_s, xs_r, rl_s, rl_r, d_s, d_r, f_s, f_r, g_s, g_r, n_s, n_r,
     a_s, a_r,
 ):
     dp = lax.axis_index("dp")
@@ -96,8 +97,9 @@
                     send(src, slot_ref(u, source), z_s.at[u, e, k], z_r.at[u, e, k], to)
 
     class Spread:
-        def __init__(self, kind, own, column, place):
+        def __init__(self, kind, own, column, place, relayed=None):
             self.kind, self.own, self.column, self.place = kind, own, column, place
+            self.relayed = relayed
 
         def on_y(self, src, slot, h, step):
             k = self.kind
@@ -109,8 +111,18 @@
             copy = remote(src, self.place(c, x, h), xs_s.at[k, j, h], xs_r.at[k, x, h],
                           (kappa * NZ + z, tn))
             local = pltpu.make_async_copy(src, self.place(c, x, h), xs_r.at[k, x, h])
-
-            @pl.when(kappa != x)
+            opposite = kappa == (x + 2) % NX
+            direct = kappa != x
+            if self.relayed is not None:
+                direct = direct & jnp.logical_not(opposite)
+                beside = ((x + (1 if h == 0 else NX - 1)) % NX) * NZ + z
+                via = remote(src, self.relayed.at[h], xs_s.at[k, j, h], rl_r.at[h], (beside, tn))
+
+                @pl.when(opposite)
+                def _():
+                    via.start()
+
+            @pl.when(direct)
             def _():
                 copy.start()
 
@@ -119,6 +131,13 @@
                 local.start()
 
             later.append((copy, kappa))
+
+        def relay(self, h):
+            step = 1 if h == 0 else NX - 1
+            source = (x + NX - step) % NX
+            arrived(self.relayed.at[h], rl_s.at[h], rl_r.at[h])
+            send(self.relayed.at[h], self.place(c, source, h), rl_s.at[h],
+                 xs_r.at[self.kind, source, h], (((x + step) % NX) * NZ + z, tn))
 
         def begin(self):
             for h in range(2):
@@ -169,6 +188,7 @@
         lambda h: text_ref.at[pl.ds(192 * h, 192)],
         lambda j, h: text_col.at[j, pl.ds(192 * h, 192)],
         lambda core, s, h: acts.at[core, s, pl.ds(192 * h, 192)],
+        text_relay,
     )
     image_spread = Spread(
         2,
@@ -180,6 +200,19 @@
     def along_x(o):
         return (((x + o) % NX) * NZ + z, tn)
 
+    barrier = pltpu.get_barrier_semaphore()
+
+    def greet_dp(o, carry):
+        pl.semaphore_signal(barrier, inc=1, device_id=((dp + o) % 32, tn), device_id_type=MESH)
+        return carry
+
+    def greet_tensor(o, carry):
+        pl.semaphore_signal(barrier, inc=1, device_id=(dp, (tn + o) % 8), device_id_type=MESH)
+        return carry
+
+    lax.fori_loop(1, 32, greet_dp, 0)
+    lax.fori_loop(1, 8, greet_tensor, 0)
+    pl.semaphore_wait(barrier, 38)
     ring(0)
     locals_ = []
     for u in range(5):
@@ -210,7 +243,59 @@
         piece = vis_ref[i].astype(F32)
         vis_own[i] = ((piece - mean) * scale * gain_ref[i] + bias_ref[i]).astype(BF)
     vis_spread.begin()
-    text_spread.begin()
+
+    class Reduce:
+        def __init__(self, index, far_out, far_in, near_out, near_in, own, value):
+            self.i, self.value, self.own = index, value, own
+            self.far_out, self.far_in = far_out, far_in
+            self.near_out, self.near_in = near_out, near_in
+            self.half = far_out.shape[0] // 2
+
+        def opposite(self):
+            i, half = self.i, self.half
+            self.far_out[...] = self.value(2).astype(BF)
+            for h in range(2):
+                part = pl.ds(half * h, half)
+                send(self.far_out.at[part], self.far_in.at[part], f_s.at[i, h], f_r.at[i, h],
+                     along_x(1 if h == 0 else 3))
+            self.own[...] = self.value(0)
+
+        def neighbours(self):
+            i, half = self.i, self.half
+            for h in range(2):
+                part = pl.ds(half * h, half)
+                rest = pl.ds(half * (1 - h), half)
+                o = 1 if h == 0 else 3
+                value = self.value(o)
+                arrived(self.far_in.at[part], f_s.at[i, h], f_r.at[i, h])
+                mine = value[half * h : half * h + half] + self.far_in[part, :].astype(F32)
+                self.near_out[h, part, :] = mine.astype(BF)
+                self.near_out[h, rest, :] = value[half * (1 - h) : half * (1 - h) + half].astype(BF)
+                send(self.near_out.at[h], self.near_in.at[h], g_s.at[i, h], g_r.at[i, h], along_x(o))
+
+        def total(self):
+            i = self.i
+            acc = self.own[...]
+            for h in range(2):
+                arrived(self.near_in.at[h], g_s.at[i, h], g_r.at[i, h])
+                acc = acc + self.near_in[h].astype(F32)
+            return acc
+
+    def project(source, u, o):
+        s = (x + o) % NX
+        first = dot(source[0, s], wq[u, 0:4].reshape(1024, 256))
+        return first + dot(source[1, s], wq[u, 4:8].reshape(1024, 256))
+
+    vis_reduce = Reduce(0, v_fo, v_fi, v_no, v_ni, v_own, lambda o: vs[(x + o) % NX])
+    image_reduce = Reduce(
+        1, i_fo, i_fi, i_no, i_ni, i_own,
+        lambda o: jnp.concatenate([project(ia, u, o) for u in range(3)], axis=1),
+    )
+    text_reduce = [
+        Reduce(2 + u, t_fo.at[u], t_fi.at[u], t_no.at[u], t_ni.at[u], t_own.at[u],
+               lambda o, u=u: project(acts, u, o))
+        for u in range(3)
+    ]
 
     def vision():
         vis_spread.from_sibling()
@@ -219,71 +304,40 @@
             for s in range(NZ):
                 term = dot(vis_all[s].reshape(NX * TOK, LANES), wp[h, s])
                 acc = term if acc is None else acc + term
-            cols = pl.ds(512 * h, 512)
-            vs[:, :, cols] = acc.reshape(NX, TOK, 512).astype(BF)
+            vs[:, :, 512 * h : 512 * h + 512] = acc.reshape(NX, TOK, 512)
+
+    def image():
+        im[...] = vis_reduce.total().astype(BF)
+        image_spread.begin()
+
+    def squares(which, source, rows):
+        for o in range(NX):
+            s = (x + o) % NX
+            acc = jnp.zeros((rows, 1), F32)
+            for core in range(2):
+                v = source[core, s].astype(F32)
+                acc = acc + jnp.sum(v * v, axis=-1, keepdims=True)
+            acc = jnp.broadcast_to(acc, (rows, 128))
+            if rows % 128:
+                acc = jnp.concatenate([acc, jnp.zeros((128 - rows % 128, 128), F32)], axis=0)
+            for b in range(acc.shape[0] // 128):
+                line = acc[128 * b : 128 * b + 128].T[0:1]
+                if o == 0:
+                    n_in[which, 0, b : b + 1, :] = line
+                else:
+                    n_out[which, o - 1, b : b + 1, :] = line
+            if o:
+                send(n_out.at[which, o - 1], n_in.at[which, o], n_s.at[which, o - 1],
+                     n_r.at[which, o - 1], along_x(o))
+
+    def row_scale(which, rows):
+        acc = n_in[which, 0]
         for o in range(1, NX):
-            send(vs.at[(x + o) % NX], vr.at[o - 1], vs_s.at[o - 1], vs_r.at[o - 1], along_x(o))
-
-    def image():
-        acc = vs[x].astype(F32)
-        for o in range(1, NX):
-            arrived(vr.at[o - 1], vs_s.at[o - 1], vs_r.at[o - 1])
-            acc = acc + vr[o - 1].astype(F32)
-        im[...] = acc.astype(BF)
-        image_spread.begin()
-
-    def squares(source, o, rows):
-        s = (x + o) % NX
-        acc = jnp.zeros((rows, 1), F32)
-        for core in range(2):
-            v = source[core, s].astype(F32)
-            acc = acc + jnp.sum(v * v, axis=-1, keepdims=True)
-        high = acc.astype(BF).astype(F32)
-        mid = (acc - high).astype(BF).astype(F32)
-        low = acc - high - mid
-        lane = lane_of((rows, 128))
-        return jnp.where(lane == 0, high, jnp.where(lane == 1, mid, low)).astype(BF)
-
-    def text_squares():
-        for o in range(NX):
-            if o == 0:
-                rstt[0] = squares(acts, 0, SEQ)
-            else:
-                stt[o - 1] = squares(acts, o, SEQ)
-        for o in range(1, NX):
-            send(stt.at[o - 1], rstt.at[o], n_s.at[0, o - 1], n_r.at[0, o - 1], along_x(o))
-
-    def image_squares():
-        for o in range(NX):
-            if o == 0:
-                rsti[0] = squares(ia, 0, TOK)
-            else:
-                sti[o - 1] = squares(ia, o, TOK)
-        for o in range(1, NX):
-            send(sti.at[o - 1], rsti.at[o], n_s.at[1, o - 1], n_r.at[1, o - 1], along_x(o))
-
-    def project(source, u, o):
-        s = (x + o) % NX
-        first = dot(source[0, s], wq[u, 0:4].reshape(1024, 256))
-        return first + dot(source[1, s], wq[u, 4:8].reshape(1024, 256))
-
-    def text_unit(u):
-        for o in (2, 1, 3, 0):
-            value = project(acts, u, o).astype(BF)
-            if o == 0:
-                rt[u, 0] = value
-            else:
-                ot[u, o - 1] = value
-                send(ot.at[u, o - 1], rt.at[u, o], t_s.at[u, o - 1], t_r.at[u, o - 1], along_x(o))
-
-    def image_unit(u):
-        for o in (2, 1, 3, 0):
-            value = project(ia, u, o).astype(BF)
-            if o == 0:
-                ri[u, 0] = value
-            else:
-                oi[u, o - 1] = value
-                send(oi.at[u, o - 1], ri.at[u, o], i_s.at[u, o - 1], i_r.at[u, o - 1], along_x(o))
+            arrived(n_in.at[which, o], n_s.at[which, o - 1], n_r.at[which, o - 1])
+            acc = acc + n_in[which, o]
+        scale = lax.rsqrt(acc / 8192.0 + decoder_epsilon)
+        lines = [jnp.broadcast_to(scale[b : b + 1], (128, 128)).T for b in range((rows + 127) // 128)]
+        return jnp.concatenate(lines, axis=0)[0:rows, 0:1]
 
     def locals_done(us):
         for u in us:
@@ -294,40 +348,47 @@
         if slot == 1:
             vis_spread.near(0)
             vis_spread.near(1)
-            text_spread.near(0)
+            text_spread.begin()
             vis_spread.far(0)
             vis_spread.far(1)
         if slot == 2:
+            text_spread.near(0)
             vis_spread.to_sibling()
+        if slot == 3:
             text_spread.near(1)
-        if slot == 3:
-            text_spread.far(0)
-            text_spread.far(1)
         if slot == 4:
             locals_done((0, 1))
             vision()
+            vis_reduce.opposite()
+            text_spread.far(0)
+            text_spread.far(1)
         if slot == 5:
-            text_spread.to_sibling()
+            vis_reduce.neighbours()
+            text_spread.relay(0)
+            text_spread.relay(1)
         if slot == 6:
             image()
-            text_spread.from_sibling()
+        if slot == 7:
             image_spread.near(0)
             image_spread.near(1)
-            text_squares()
             image_spread.far(0)
             image_spread.far(1)
-        if slot == 7:
+            text_spread.to_sibling()
+            text_spread.from_sibling()
             locals_done((2, 3, 4))
-            text_unit(0)
+            text_reduce[0].opposite()
+        if slot == 8:
             image_spread.to_sibling()
+            text_reduce[0].neighbours()
+            text_reduce[1].opposite()
+            squares(0, acts, SEQ)
         if slot == 9:
+            text_reduce[1].neighbours()
             image_spread.from_sibling()
-            text_unit(1)
-            image_squares()
-            image_unit(0)
-            image_unit(1)
-        if slot == 11:
-            image_unit(2)
+            squares(1, ia, TOK)
+            image_reduce.opposite()
+            text_reduce[2].opposite()
+            image_reduce.neighbours()
 
     first = jnp.int32(0)
     my_first = jnp.int32(0)
@@ -347,23 +408,9 @@
     same = ((row >> 4) == owner) & (((row >> 3) & 1) == (col >> 6)) & ((row & 7) == (col & 7))
     pick = jnp.where(same, 1.0, 0.0).astype(BF)
 
-    def gathered(buffer, rows, sems, receives):
-        acc = buffer[0].astype(F32)
-        for o in range(1, NX):
-            arrived(buffer.at[o], sems.at[o - 1], receives.at[o - 1])
-            acc = acc + buffer[o].astype(F32)
-        return acc
-
-    def row_scale(buffer, rows, which):
-        acc = gathered(buffer, rows, n_s.at[which], n_r.at[which])
-        total = jnp.sum(jnp.where(lane_of(acc.shape) < 3, acc, 0.0), axis=-1, keepdims=True)
-        return lax.rsqrt(total / 8192.0 + decoder_epsilon)
-
-    image_scale = row_scale(rsti, TOK, 1)
-    pieces = [(gathered(ri.at[u], TOK, i_s.at[u], i_r.at[u]) * image_scale).astype(BF)
-              for u in range(3)]
-    low = jnp.concatenate([pieces[0], pieces[1][:, 0:128]], axis=1)
-    high = jnp.concatenate([pieces[1][:, 128:256], pieces[2]], axis=1)
+    image_scale = row_scale(1, TOK)
+    image_rows = (image_reduce.total() * image_scale).astype(BF)
+    low, high = image_rows[:, 0:384], image_rows[:, 384:768]
     both = jnp.concatenate([low, high], axis=0)
     a2s[...] = dot(pick, both).astype(BF).reshape(32, 16, 384)
     a2r[dp] = a2s[dp]
@@ -374,7 +421,7 @@
         return carry
 
     lax.fori_loop(1, 32, route, 0)
-    text_unit(2)
+    text_reduce[2].neighbours()
 
     shape = (SEQ, 512)
     row, col = row_of(shape), lane_of(shape)
@@ -387,7 +434,7 @@
     place = row_of((SEQ, 128)) - off_ref[0]
     is_image = (place >= 0) & (place < 8 * my_count)
     causal = row_of((SEQ, SEQ)) >= lane_of((SEQ, SEQ))
-    text_scale = row_scale(rstt, SEQ, 0)
+    text_scale = row_scale(0, SEQ)
 
     def route_done(o, carry):
         source = (dp - o + 32) % 32
@@ -399,7 +446,7 @@
     image_low = dot(sel_low, routed)
     image_high = dot(sel_high, routed)
 
-    texts = [gathered(rt.at[u], SEQ, t_s.at[u], t_r.at[u]) * text_scale for u in range(3)]
+    texts = [text_reduce[u].total() * text_scale for u in range(3)]
     cos, sin = cos_ref[...], sin_ref[...]
 
     def column(i):
@@ -485,23 +532,32 @@
             pltpu.VMEM((4, TOK, LANES), BF),
             pltpu.VMEM((8, TOK, 128), F32),
             pltpu.VMEM((2, NX, SEQ, 1024), BF),
-            pltpu.VMEM((NX, TOK, 1024), BF),
-            pltpu.VMEM((NX - 1, TOK, 1024), BF),
+            pltpu.VMEM((NX, TOK, 1024), F32),
             pltpu.VMEM((TOK, 1024), BF),
             pltpu.VMEM((2, NX, TOK, 1024), BF),
-            pltpu.VMEM((3, NX - 1, SEQ, 256), BF),
-            pltpu.VMEM((3, NX, SEQ, 256), BF),
-            pltpu.VMEM((3, NX - 1, TOK, 256), BF),
-            pltpu.VMEM((3, NX, TOK, 256), BF),
-            pltpu.VMEM((NX - 1, SEQ, 128), BF),
-            pltpu.VMEM((NX, SEQ, 128), BF),
-            pltpu.VMEM((NX - 1, TOK, 128), BF),
-            pltpu.VMEM((NX, TOK, 128), BF),
+            pltpu.VMEM((2, NX - 1, 8, 128), F32),
+            pltpu.VMEM((2, NX, 8, 128), F32),
+            pltpu.VMEM((TOK, 1024), BF),
+            pltpu.VMEM((TOK, 1024), BF),
+            pltpu.VMEM((2, TOK, 1024), BF),
+            pltpu.VMEM((2, TOK, 1024), BF),
+            pltpu.VMEM((TOK, 1024), F32),
+            pltpu.VMEM((TOK, 768), BF),
+            pltpu.VMEM((TOK, 768), BF),
+            pltpu.VMEM((2, TOK, 768), BF),
+            pltpu.VMEM((2, TOK, 768), BF),
+            pltpu.VMEM((TOK, 768), F32),
+            pltpu.VMEM((3, SEQ, 256), BF),
+            pltpu.VMEM((3, SEQ, 256), BF),
+            pltpu.VMEM((3, 2, SEQ, 256), BF),
+            pltpu.VMEM((3, 2, SEQ, 256), BF),
+            pltpu.VMEM((3, SEQ, 256), F32),
             pltpu.VMEM((32, 16, 384), BF),
             pltpu.VMEM((32, 16, 384), BF),
             pltpu.VMEM((3, 4, TOK, LANES), BF),
             pltpu.VMEM((3, SEQ, 1024), BF),
             pltpu.VMEM((3, TOK, 1024), BF),
+            pltpu.VMEM((2, 192, 1024), BF),
             dma((5,)),
             dma((5, 2, 4)),
             dma((5, 2, 4)),
@@ -511,20 +567,20 @@
             dma((3, 3, 2)),
             dma((3, 4, 2)),
             dma((3, NX, 2)),
+            dma((2,)),
+            dma((2,)),
             dma((3, NX, 2)),
             dma((3, NX, 2)),
-            dma((3,)),
-            dma((3,)),
-            dma((3, 3)),
-            dma((3, 3)),
-            dma((3, 3)),
-            dma((3, 3)),
+            dma((5, 2)),
+            dma((5, 2)),
+            dma((5, 2)),
+            dma((5, 2)),
             dma((2, 3)),
             dma((2, 3)),
             dma((31,)),
             dma((31,)),
         ],
-        compiler_params=pltpu.CompilerParams(has_side_effects=True, vmem_limit_bytes=60 << 20),
+        compiler_params=pltpu.CompilerParams(collective_id=0, has_side_effects=True, vmem_limit_bytes=60 << 20),
         name="step",
     )(tile_counts, image_offsets, vis, features(ln_gain), features(ln_bias), proj, qkv,
       text_rows[0], jnp.asarray(cos), jnp.asarray(sin))

time: 180 us -> 142 us (0.79)
  Pallas kernels: 169 us -> 130 us
    pallas_call x1, Pallas kernels: 169 us -> 130 us  [per_device(): pl.pallas_call(kernel, out_shape=jax.ShapeDtypeStruct((SEQ, 512), BF), in...]
where the time goes in v3:
time: 142 us; the launch traced here: 141 us
  Pallas kernels  130 us (92%)
  local copies, waits for them, and re-layouts  8.77 us (6%)
    pallas_call x1, Pallas kernels, per_device(): pl.pallas_call(kernel, out_shape=jax.ShapeDtypeStruct((SEQ, 512), BF), in...  130 us
    unnamed x11, local copies, waits for them, and re-layouts  3.04 us

profile of v3, /device:TPU:8, one launch (start us, length us, event | category | flops | bytes accessed | tf_op | source)
XLA Modules:
  0.0 140.9 jit_solution(16246743990249218902)
XLA Ops:
  0.0 0.0 copy-start.1
  0.0 0.8 constant_dynamic-slice_fusion
  0.8 0.1 reshape.39
  0.9 0.2 copy.16
  1.1 0.1 copy.17
  1.1 0.6 pad.16.gain_ref
  1.8 0.1 reshape.41
  1.8 0.1 copy.18
  2.0 0.1 copy.19
  2.1 0.6 pad.17.bias_ref
  2.7 0.8 dynamic_slice.11
  3.4 0.0 copy-done.1
  3.5 0.0 copy-start.2
  3.5 0.1 copy.22
  3.6 0.8 copy-done.2
  4.4 0.1 copy.21
  4.5 0.2 copy.23
  4.7 0.0 copy-start
  4.7 0.9 fusion.qkv_ref
  5.6 0.1 copy-done
  5.7 0.2 reshape.43
  5.9 0.0 copy-start.3
  5.9 0.8 copy.26
  6.7 0.1 copy-done.3
  6.8 0.1 reshape.37
  7.0 0.2 copy.14
  7.2 0.1 copy.15
  7.3 0.7 pad.15.vis_ref
  8.6 130.5 %step.1 = bf16[384,512]{1,0:T(8,128)(2,1)} custom-call(s32[32]{0:T(128)} %cnt_ref.1, s32[1]{0:T(128)S(6)} %copy.28.off_ref, bf16[4,64,256]{2,1,0:T(8,128)(2,1)} %pad.15.vis_ref, f32[4,1,256]{2,1,0:T(1,128)} %pad.16.gain_ref, f32[4,1,256]{2,1,0:T(1,128)} %pad.17.bias_ref, bf16[2,208,512]{2,1,0:T(8,128)(2,1)} %bitcast.21, bf16[3,256,256]{2,1,0:T(8,128)(2,1)} %fusion.qkv_ref, ...), custom_call_target="tpu_custom_call" | custom-call | tf_op jit(solution)/shard_map/step/pallas_call | solution.py:523
  139.1 1.8 %copy.29 = bf16[1,384,512]{2,1,0:T(8,128)(2,1)} copy(bf16[1,384,512]{2,1,0:T(8,128)(2,1)} %bitcast.23) | data formatting | bytes 786432
  (2 shorter events, 0.1 us)
Async XLA Ops:
  0.0 3.5 %copy-start.1 = (bf16[256,512]{1,0:T(8,128)(2,1)S(1)}, bf16[256,512]{1,0:T(8,128)(2,1)}, u32[]{:S(2)}) copy-start(bf16[256,512]{1,0:T(8,128)(2,1)} %param.18) | copy-start | bytes 786436
  3.5 0.9 copy-start.2
  4.7 1.0 copy-start
  5.9 0.9 copy-start.3

commit v4 on v3

v4 whole, which is shorter than its diff:
```python
import functools

import jax
import jax.numpy as jnp
import numpy as np
from jax import lax
from jax.experimental import pallas as pl
from jax.experimental.pallas import tpu as pltpu
from jax.sharding import PartitionSpec as P

MESH = pl.DeviceIdType.MESH
BF = jnp.bfloat16
F32 = jnp.float32

HEAD_WIDTH = 128
SEQ = 384
TOK = 64
CHUNKS = 4
NX, NY, NZ = 4, 4, 8
LANES = 256
ROWS = 208
PART = 200
vision_epsilon = 1e-06
decoder_epsilon = 1e-05
rope_base = 500000.0

STARTS = (0, 0, 2, 3, 4)
SLOTS = max(STARTS) + 5


def dot(a, b):
    return jnp.dot(a, b, preferred_element_type=F32)


def lane_of(shape):
    return lax.broadcasted_iota(jnp.int32, shape, len(shape) - 1)


def row_of(shape):
    return lax.broadcasted_iota(jnp.int32, shape, len(shape) - 2)


def kernel(
    cnt_ref, off_ref, vis_ref, affine_ref, proj_ref, qkv_ref, raw_ref, attn_ref, cos_ref, sin_ref,
    out_ref,
    wp, wq, vis_all, vis_own, stats, image_stats, text_ref, pick_ref, sel_ref, acts, vs, im, ia,
    v_fo, v_fi, v_no, v_ni, v_own, i_fo, i_fi, i_no, i_ni, i_own, t_fo, t_fi, t_no, t_ni, t_own,
    a2s, a2r, vis_col, text_mid, im_col, relay_y, relay_x,
    l_sem, z_s, z_r, st_s, st_r, ys_s, ys_r, xs_s, xs_r, tx_s, tx_r, d_s, d_r, f_s, f_r, g_s, g_r, n_s, n_r,
    a_s, a_r,
):
    dp = lax.axis_index("dp")
    tn = lax.axis_index("tensor")
    x, z = dp // NZ, dp % NZ
    y, c = tn // 2, tn % 2
    pending = []

    def remote(src, dst, ssem, rsem, to):
        return pltpu.make_async_remote_copy(
            src_ref=src, dst_ref=dst, send_sem=ssem, recv_sem=rsem, device_id=to,
            device_id_type=MESH,
        )

    def send(src, dst, ssem, rsem, to):
        copy = remote(src, dst, ssem, rsem, to)
        copy.start()
        pending.append(copy)

    here = (dp, tn)

    def arrived(ref, ssem, rsem):
        remote(ref, ref, ssem, rsem, here).wait_recv()

    def own(u):
        return proj_ref.at[u] if u < 2 else qkv_ref.at[u - 2]

    def slot_ref(u, source):
        if u < 2:
            return wp.at[u, source, pl.ds(0, ROWS)]
        return wq.at[u - 2, source]

    def goes(u, e, k):
        return k < 4 or (u % 2 == e)

    def ring(slot):
        for u, start in enumerate(STARTS):
            k = slot - start
            if k < 0 or k > 4:
                continue
            for e in range(2):
                sign = 1 if e == 0 else -1
                source = (z - sign * k + 2 * NZ) % NZ
                if k >= 1 and goes(u, e, k):
                    arrived(slot_ref(u, source), z_s.at[u, e, k - 1], z_r.at[u, e, k - 1])
                if k <= 3 and goes(u, e, k + 1):
                    to = (x * NZ + (z + sign + NZ) % NZ, tn)
                    src = own(u) if k == 0 else slot_ref(u, source)
                    send(src, slot_ref(u, source), z_s.at[u, e, k], z_r.at[u, e, k], to)

    class Spread:
        def __init__(self, kind, own, column, place):
            self.kind, self.own, self.column, self.place = kind, own, column, place

        def on_y(self, src, slot, h, step):
            k = self.kind
            send(src, self.column(slot, h), ys_s.at[k, slot, h], ys_r.at[k, slot, h],
                 (dp, ((y + step + NY) % NY) * 2 + c))

        def on_x(self, src, j, h, kappa):
            k = self.kind
            copy = remote(src, self.place(c, x, h), xs_s.at[k, j, h], xs_r.at[k, x, h],
                          (kappa * NZ + z, tn))
            local = pltpu.make_async_copy(src, self.place(c, x, h), xs_r.at[k, x, h])

            @pl.when(kappa != x)
            def _():
                copy.start()

            @pl.when(kappa == x)
            def _():
                local.start()

            later.append((copy, kappa != x))

        def begin_y(self):
            for h in range(2):
                self.on_y(self.own(h), 0, h, 1)
                self.on_y(self.own(h), 1, h, -1)

        def begin_x(self):
            for h in range(2):
                self.on_x(self.own(h), 3, h, y)

        def near(self, h):
            k = self.kind
            for slot, step in ((0, 1), (1, -1)):
                arrived(self.column(slot, h), ys_s.at[k, slot, h], ys_r.at[k, slot, h])
                if slot == h:
                    src = self.column(slot, h)
                    send(src, self.column(2, h), ys_s.at[k, 2, h], ys_r.at[k, 2, h],
                         (dp, ((y + step + NY) % NY) * 2 + c))
            for slot, step in ((0, 1), (1, -1)):
                self.on_x(self.column(slot, h), slot, h, (y - step + NY) % NY)

        def far(self, h):
            k = self.kind
            arrived(self.column(2, h), ys_s.at[k, 2, h], ys_r.at[k, 2, h])
            self.on_x(self.column(2, h), 2, h, (y + 2) % NY)

        def to_sibling(self, offsets=(0, 1, 3, 2)):
            k = self.kind
            for o in offsets:
                s = (x + o) % NX
                for h in range(2):
                    ref = self.place(c, s, h)
                    arrived(ref, xs_s.at[k, 0, h], xs_r.at[k, s, h])
                    send(ref, ref, d_s.at[k, s, h], d_r.at[k, s, h], (dp, tn + 1 - 2 * c))

        def from_sibling(self):
            k = self.kind
            for s in range(NX):
                for h in range(2):
                    arrived(self.place(1 - c, s, h), d_s.at[k, s, h], d_r.at[k, s, h])

    later = []
    vis_spread = Spread(
        0,
        lambda h: vis_own.at[pl.ds(2 * h, 2)],
        lambda j, h: vis_col.at[j, pl.ds(2 * h, 2)],
        lambda core, s, h: vis_all.at[pl.ds(4 * core + 2 * h, 2), s],
    )
    def crossed(a, b):
        return ((a // 2 + b // 2) % 2) * 2 + (a + b) % 2

    class TextSpread:
        def part(self, q):
            return pl.ds(q * (SEQ // CHUNKS), SEQ // CHUNKS)

        def block(self, core, step, q):
            return acts.at[core, crossed(x, (y + step + NY) % NY), self.part(q)]

        def hop(self, q, at, src, dst, relay, kind, along):
            other = x if along == "y" else y

            def device(place):
                return (dp, place * 2 + c) if along == "y" else (place * NZ + z, tn)

            ssem, rsem = tx_s.at[kind, q], tx_r.at[kind, q]
            straight = remote(src, dst, ssem, rsem, device(crossed(at, other)))
            local = pltpu.make_async_copy(src, dst, rsem)
            beside = device((at + (1 if q % 2 == 0 else 3)) % 4)
            via = remote(src, relay.at[q], ssem, tx_r.at[kind + 1, q], beside)

            @pl.when(other == 0)
            def _():
                local.start()

            @pl.when((other == 1) | (other == 3))
            def _():
                straight.start()

            @pl.when(other == 2)
            def _():
                via.start()

            later.append((straight, other != 0))

        def relay(self, q, at, dst, relay, kind, along):
            other = x if along == "y" else y
            nxt = (at + (1 if q % 2 == 0 else 3)) % 4
            to = (dp, nxt * 2 + c) if along == "y" else (nxt * NZ + z, tn)
            on = remote(relay.at[q], dst, tx_s.at[kind + 1, q], tx_r.at[kind, q], to)

            @pl.when(other == 2)
            def _():
                remote(relay.at[q], relay.at[q], tx_s.at[kind + 1, q], tx_r.at[kind + 1, q],
                       here).wait_recv()
                on.start()

            later.append((on, other == 2))

        def begin(self):
            for q in range(CHUNKS):
                self.hop(q, y, text_ref.at[self.part(q)], text_mid.at[self.part(q)], relay_y, 0, "y")

        def pass_y(self, q):
            self.relay(q, y, text_mid.at[self.part(q)], relay_y, 0, "y")

        def turn(self, q):
            mid = text_mid.at[self.part(q)]
            arrived(mid, tx_s.at[0, q], tx_r.at[0, q])
            self.hop(q, x, mid, acts.at[c, x, self.part(q)], relay_x, 2, "x")

        def pass_x(self, q):
            source = (x + (3 if q % 2 == 0 else 1)) % NX
            self.relay(q, x, acts.at[c, source, self.part(q)], relay_x, 2, "x")

        def on_y(self, q, block_step, step, kind):
            ref = self.block(c, block_step, q)
            send(ref, ref, tx_s.at[kind, q], tx_r.at[kind, q], (dp, ((y + step + NY) % NY) * 2 + c))

        def to_other(self, q, j, step):
            ref = self.block(c, step, q)
            send(ref, ref, d_s.at[1, j, q], d_r.at[1, j, q], (dp, tn + 1 - 2 * c))

        def mine(self, q):
            arrived(self.block(c, 0, q), tx_s.at[2, q], tx_r.at[2, q])
            self.on_y(q, 0, 1, 4)
            self.on_y(q, 0, -1, 5)
            self.to_other(q, 0, 0)

        def near(self, q):
            arrived(self.block(c, -1, q), tx_s.at[4, q], tx_r.at[4, q])
            arrived(self.block(c, 1, q), tx_s.at[5, q], tx_r.at[5, q])
            if q % 2 == 0:
                self.on_y(q, -1, 1, 6)
            else:
                self.on_y(q, 1, -1, 6)
            self.to_other(q, 1, -1)
            self.to_other(q, 2, 1)

        def far(self, q):
            arrived(self.block(c, 2, q), tx_s.at[6, q], tx_r.at[6, q])
            self.to_other(q, 3, 2)

        def from_sibling(self):
            for q in range(CHUNKS):
                for j, step in enumerate((0, -1, 1, 2)):
                    arrived(self.block(1 - c, step, q), d_s.at[1, j, q], d_r.at[1, j, q])

    text_spread = TextSpread()
    image_spread = Spread(
        2,
        lambda h: im.at[pl.ds(32 * h, 32)],
        lambda j, h: im_col.at[j, pl.ds(32 * h, 32)],
        lambda core, s, h: ia.at[core, s, pl.ds(32 * h, 32)],
    )

    def along_x(o):
        return (((x + o) % NX) * NZ + z, tn)

    barrier = pltpu.get_barrier_semaphore()

    def greet_dp(o, carry):
        pl.semaphore_signal(barrier, inc=1, device_id=((dp + o) % 32, tn), device_id_type=MESH)
        return carry

    def greet_tensor(o, carry):
        pl.semaphore_signal(barrier, inc=1, device_id=(dp, (tn + o) % 8), device_id_type=MESH)
        return carry

    lax.fori_loop(1, 32, greet_dp, 0)
    lax.fori_loop(1, 8, greet_tensor, 0)

    for u in range(2):
        for s in range(NZ):
            wp[u, s, ROWS:LANES, :] = jnp.zeros((LANES - ROWS, 512), BF)
    locals_ = []
    for u in range(5):
        local = pltpu.make_async_copy(own(u), slot_ref(u, z), l_sem.at[u])
        local.start()
        locals_.append(local)

    def lines_of(column):
        rows = column.shape[0]
        wide = jnp.broadcast_to(column, (rows, 128))
        if rows % 128:
            wide = jnp.concatenate([wide, jnp.zeros((128 - rows % 128, 128), F32)], axis=0)
        return [wide[128 * b : 128 * b + 128].T[0:1] for b in range(wide.shape[0] // 128)]

    def column_of(lines, rows):
        wide = [jnp.broadcast_to(line, (128, 128)).T for line in lines]
        wide = wide[0] if len(wide) == 1 else jnp.concatenate(wide, axis=0)
        return wide[0:rows, 0:1]

    xv = vis_ref[...].astype(F32)
    mean = jnp.sum(jnp.sum(xv, axis=0), axis=-1, keepdims=True) / (4 * PART)
    centred = jnp.where(lane_of(xv.shape) < PART, xv - mean[None], 0.0)
    m2 = jnp.sum(jnp.sum(centred * centred, axis=0), axis=-1, keepdims=True)
    raw = raw_ref[...].astype(F32)
    lines = lines_of(jnp.sum(raw * raw, axis=-1, keepdims=True)) + lines_of(mean) + lines_of(m2)
    stats[tn] = jnp.concatenate(lines + [jnp.zeros((3, 128), F32)], axis=0)

    first = jnp.int32(0)
    my_first = jnp.int32(0)
    my_count = jnp.int32(0)
    owners = [jnp.int32(0)] * 8
    for s in range(NX * NZ):
        count = cnt_ref[s]
        my_first = my_first + jnp.where(s < dp, count, 0)
        my_count = my_count + jnp.where(s == dp, count, 0)
        first = first + count
        owners = [a + jnp.where(first <= r * 32 + dp, 1, 0) for r, a in enumerate(owners)]
    shape = (512, 128)
    row, col = row_of(shape), lane_of(shape)
    owner = jnp.zeros(shape, jnp.int32)
    for r in range(8):
        owner = jnp.where(((col >> 3) & 7) == r, owners[r], owner)
    same = ((row >> 4) == owner) & (((row >> 3) & 1) == (col >> 6)) & ((row & 7) == (col & 7))
    pick_ref[...] = jnp.where(same, 1.0, 0.0).astype(BF)
    shape = (SEQ, 512)
    row, col = row_of(shape), lane_of(shape)
    place = row - off_ref[0]
    inside = (place >= 0) & (place < 8 * my_count)
    source = (my_first + (place >> 3)) & 31
    match = inside & ((col >> 4) == source) & ((col & 7) == (place & 7))
    for h in range(2):
        chosen = match & (((col >> 3) & 1) == h)
        sel_ref[h] = jnp.where(chosen, 1.0, 0.0).astype(BF)
    place = row_of((SEQ, 128)) - off_ref[0]
    is_image = (place >= 0) & (place < 8 * my_count)

    pl.semaphore_wait(barrier, 38)
    for o in range(1, 8):
        send(stats.at[tn], stats.at[tn], st_s.at[o - 1], st_r.at[o - 1], (dp, (tn + o) % 8))
    ring(0)
    for o in range(1, 8):
        arrived(stats.at[(tn - o + 8) % 8], st_s.at[o - 1], st_r.at[o - 1])
    means = [stats[t][3:4] for t in range(8)]
    mean = sum(means[1:], means[0]) / 8.0
    total = jnp.zeros((1, 128), F32)
    for t in range(8):
        apart = means[t] - mean
        total = total + stats[t][4:5] + (4.0 * PART) * apart * apart
    scale = column_of([lax.rsqrt(total / (32.0 * PART) + vision_epsilon)], TOK)
    mean = column_of([mean], TOK)
    for i in range(4):
        piece = vis_ref[i].astype(F32)
        vis_own[i] = ((piece - mean) * scale * affine_ref[0, i] + affine_ref[1, i]).astype(BF)
    vis_spread.begin_y()
    vis_spread.begin_x()
    total = stats[0]
    for t in range(1, 8):
        total = total + stats[t]
    scale = lax.rsqrt(total / 8192.0 + decoder_epsilon)
    scale = column_of([scale[b : b + 1] for b in range(3)], SEQ)
    gain = attn_ref[:, pl.ds(pl.multiple_of(tn * 1024, 1024), 1024)]
    text_ref[...] = (raw_ref[...].astype(F32) * scale * gain).astype(BF)
    text_spread.begin()

    class Reduce:
        def __init__(self, index, far_out, far_in, near_out, near_in, own, value):
            self.i, self.value, self.own = index, value, own
            self.far_out, self.far_in = far_out, far_in
            self.near_out, self.near_in = near_out, near_in
            self.half = far_out.shape[0] // 2

        def opposite(self):
            i, half = self.i, self.half
            self.far_out[...] = self.value(2).astype(BF)
            for h in range(2):
                part = pl.ds(half * h, half)
                send(self.far_out.at[part], self.far_in.at[part], f_s.at[i, h], f_r.at[i, h],
                     along_x(1 if h == 0 else 3))
            self.own[...] = self.value(0)

        def neighbours(self):
            i, half = self.i, self.half
            for h in range(2):
                part = pl.ds(half * h, half)
                rest = pl.ds(half * (1 - h), half)
                o = 1 if h == 0 else 3
                value = self.value(o)
                arrived(self.far_in.at[part], f_s.at[i, h], f_r.at[i, h])
                mine = value[half * h : half * h + half] + self.far_in[part, :].astype(F32)
                self.near_out[h, part, :] = mine.astype(BF)
                self.near_out[h, rest, :] = value[half * (1 - h) : half * (1 - h) + half].astype(BF)
                send(self.near_out.at[h], self.near_in.at[h], g_s.at[i, h], g_r.at[i, h], along_x(o))

        def total(self):
            i = self.i
            acc = self.own[...]
            for h in range(2):
                arrived(self.near_in.at[h], g_s.at[i, h], g_r.at[i, h])
                acc = acc + self.near_in[h].astype(F32)
            return acc

    def project(source, u, o):
        s = (x + o) % NX
        first = dot(source[0, s], wq[u, 0:4].reshape(1024, 256))
        return first + dot(source[1, s], wq[u, 4:8].reshape(1024, 256))

    vis_reduce = Reduce(0, v_fo, v_fi, v_no, v_ni, v_own, lambda o: vs[(x + o) % NX])
    image_reduce = Reduce(
        1, i_fo, i_fi, i_no, i_ni, i_own,
        lambda o: jnp.concatenate([project(ia, u, o) for u in range(3)], axis=1),
    )
    text_reduce = [
        Reduce(2 + u, t_fo.at[u], t_fi.at[u], t_no.at[u], t_ni.at[u], t_own.at[u],
               lambda o, u=u: project(acts, u, o))
        for u in range(3)
    ]

    def vision():
        vis_spread.from_sibling()
        for h in range(2):
            acc = None
            for s in range(NZ):
                term = dot(vis_all[s].reshape(NX * TOK, LANES), wp[h, s])
                acc = term if acc is None else acc + term
            vs[:, :, 512 * h : 512 * h + 512] = acc.reshape(NX, TOK, 512)

    def image():
        tokens = vis_reduce.total().astype(BF).astype(F32)
        lines = lines_of(jnp.sum(tokens * tokens, axis=-1, keepdims=True))
        image_stats[tn] = jnp.concatenate(lines + [jnp.zeros((7, 128), F32)], axis=0)
        im[...] = (tokens * gain).astype(BF)
        image_spread.begin_y()
        image_spread.begin_x()
        for o in range(1, 8):
            send(image_stats.at[tn], image_stats.at[tn], n_s.at[o - 1], n_r.at[o - 1],
                 (dp, (tn + o) % 8))

    def locals_done(us):
        for u in us:
            locals_[u].wait()

    vis_spread.near(0)
    vis_spread.near(1)
    ring(1)
    text_spread.pass_y(0)
    text_spread.pass_y(1)
    text_spread.turn(0)
    text_spread.turn(1)
    ring(2)
    text_spread.pass_y(2)
    text_spread.pass_y(3)
    text_spread.turn(2)
    text_spread.turn(3)
    vis_spread.far(0)
    vis_spread.far(1)
    text_spread.pass_x(0)
    text_spread.pass_x(1)
    text_spread.mine(0)
    text_spread.mine(1)
    ring(3)
    text_spread.pass_x(2)
    text_spread.pass_x(3)
    text_spread.mine(2)
    text_spread.mine(3)
    vis_spread.to_sibling()
    text_spread.near(0)
    ring(4)
    locals_done((0, 1))
    vision()
    vis_reduce.opposite()
    text_spread.near(1)
    text_spread.near(2)
    vis_reduce.neighbours()
    text_spread.near(3)
    ring(5)
    text_spread.far(0)
    text_spread.far(1)
    image()
    ring(6)
    text_spread.far(2)
    text_spread.far(3)
    image_spread.near(0)
    image_spread.near(1)
    text_spread.from_sibling()
    locals_done((2, 3, 4))
    text_reduce[0].opposite()
    ring(7)
    image_spread.far(0)
    image_spread.far(1)
    text_reduce[1].opposite()
    text_reduce[0].neighbours()
    ring(8)
    image_spread.to_sibling()
    text_reduce[2].opposite()
    image_spread.from_sibling()
    image_reduce.opposite()
    text_reduce[1].neighbours()
    image_reduce.neighbours()
    text_reduce[2].neighbours()

    total = image_stats[tn]
    for o in range(1, 8):
        source = (tn - o + 8) % 8
        arrived(image_stats.at[source], n_s.at[o - 1], n_r.at[o - 1])
        total = total + image_stats[source]
    image_scale = column_of([lax.rsqrt(total[0:1] / 8192.0 + decoder_epsilon)], TOK)
    image_rows = (image_reduce.total() * image_scale).astype(BF)
    low, high = image_rows[:, 0:384], image_rows[:, 384:768]
    both = jnp.concatenate([low, high], axis=0)
    a2s[...] = dot(pick_ref[...], both).astype(BF).reshape(32, 16, 384)
    a2r[dp] = a2s[dp]

    def route(o, carry):
        to = (dp + o) % 32
        remote(a2s.at[to], a2r.at[dp], a_s.at[o - 1], a_r.at[o - 1], (to, tn)).start()
        return carry

    lax.fori_loop(1, 32, route, 0)

    causal = row_of((SEQ, SEQ)) >= lane_of((SEQ, SEQ))

    def route_done(o, carry):
        source = (dp - o + 32) % 32
        remote(a2s.at[source], a2r.at[source], a_s.at[o - 1], a_r.at[o - 1], here).wait_recv()
        return carry

    lax.fori_loop(1, 32, route_done, 0)
    routed = a2r[...].reshape(512, 384)
    image_low = dot(sel_ref[0], routed)
    image_high = dot(sel_ref[1], routed)

    texts = [text_reduce[u].total() for u in range(3)]
    cos, sin = cos_ref[...], sin_ref[...]

    def column(i):
        text = texts[i // 2][:, 128 * (i % 2) : 128 * (i % 2) + 128]
        picture = image_low if i < 3 else image_high
        picture = picture[:, 128 * (i % 3) : 128 * (i % 3) + 128]
        return jnp.where(is_image, picture, text)

    def turned(value):
        return (value * cos + pltpu.roll(value, 64, 1) * sin).astype(BF)

    key = turned(column(4))
    value = column(5).astype(BF)
    for h in range(4):
        query = turned(column(h))
        scores = lax.dot_general(query, key, (((1,), (1,)), ((), ())), preferred_element_type=F32)
        scores = jnp.where(causal, scores * HEAD_WIDTH ** (-0.5), -1e30)
        powers = jnp.exp(scores - jnp.max(scores, axis=-1, keepdims=True))
        weights = (powers / jnp.sum(powers, axis=-1, keepdims=True)).astype(BF)
        out_ref[:, 128 * h : 128 * h + 128] = dot(weights, value).astype(BF)

    for copy in pending:
        copy.wait_send()
    for copy, went in later:

        @pl.when(went)
        def _(copy=copy):
            copy.wait_send()


    def sent(o, carry):
        to = (dp + o) % 32
        remote(a2s.at[to], a2r.at[dp], a_s.at[o - 1], a_r.at[o - 1], here).wait_send()
        return carry

    lax.fori_loop(1, 32, sent, 0)


def rotation_tables():
    exponents = np.arange(64, dtype=np.float32) * np.float32(2.0 / 128)
    frequency = np.float32(rope_base) ** (-exponents)
    angles = np.arange(SEQ, dtype=np.float32)[:, None] * frequency[None, :]
    cos, sin = np.cos(angles), np.sin(angles)
    return (
        np.concatenate([cos, cos], axis=1).astype(np.float32),
        np.concatenate([-sin, sin], axis=1).astype(np.float32),
    )


def per_device(vis_rows, ln_gain, ln_bias, proj_weight, text_rows, attn_gain, w_query,
               key_value_weight, tile_counts, image_offsets):
    tn = lax.axis_index("tensor")

    def lanes(a):
        return jnp.pad(a, [(0, 0)] * (a.ndim - 1) + [(0, LANES - PART)])

    vis = vis_rows.reshape(TOK, 2, 4, 100).transpose(2, 0, 3, 1).reshape(4, TOK, PART)
    vis = lanes(vis)

    affine = jnp.stack([ln_gain, ln_bias])
    affine = lax.dynamic_slice_in_dim(affine, tn * 400, 400, 2)
    affine = lanes(affine.reshape(2, 2, 4, 100).transpose(0, 2, 3, 1).reshape(2, 4, 1, PART))

    proj = jnp.pad(proj_weight.reshape(PART, 1024), ((0, ROWS - PART), (0, 0)))
    proj = proj.reshape(ROWS, 2, 512).transpose(1, 0, 2)
    qkv = jnp.concatenate([w_query, key_value_weight.reshape(256, 256)], axis=1)
    qkv = qkv.reshape(256, 3, 256).transpose(1, 0, 2)
    cos, sin = rotation_tables()
    vmem = pl.BlockSpec(memory_space=pltpu.VMEM)
    smem = pl.BlockSpec(memory_space=pltpu.SMEM)
    dma = pltpu.SemaphoreType.DMA
    out = pl.pallas_call(
        kernel,
        out_shape=jax.ShapeDtypeStruct((SEQ, 512), BF),
        in_specs=[smem, smem] + [vmem] * 8,
        out_specs=vmem,
        scratch_shapes=[
            pltpu.VMEM((2, NZ, LANES, 512), BF),
            pltpu.VMEM((3, NZ, 256, 256), BF),
            pltpu.VMEM((NZ, NX, TOK, LANES), BF),
            pltpu.VMEM((4, TOK, LANES), BF),
            pltpu.VMEM((8, 8, 128), F32),
            pltpu.VMEM((8, 8, 128), F32),
            pltpu.VMEM((SEQ, 1024), BF),
            pltpu.VMEM((512, 128), BF),
            pltpu.VMEM((2, SEQ, 512), BF),
            pltpu.VMEM((2, NX, SEQ, 1024), BF),
            pltpu.VMEM((NX, TOK, 1024), F32),
            pltpu.VMEM((TOK, 1024), BF),
            pltpu.VMEM((2, NX, TOK, 1024), BF),
            pltpu.VMEM((TOK, 1024), BF),
            pltpu.VMEM((TOK, 1024), BF),
            pltpu.VMEM((2, TOK, 1024), BF),
            pltpu.VMEM((2, TOK, 1024), BF),
            pltpu.VMEM((TOK, 1024), F32),
            pltpu.VMEM((TOK, 768), BF),
            pltpu.VMEM((TOK, 768), BF),
            pltpu.VMEM((2, TOK, 768), BF),
            pltpu.VMEM((2, TOK, 768), BF),
            pltpu.VMEM((TOK, 768), F32),
            pltpu.VMEM((3, SEQ, 256), BF),
            pltpu.VMEM((3, SEQ, 256), BF),
            pltpu.VMEM((3, 2, SEQ, 256), BF),
            pltpu.VMEM((3, 2, SEQ, 256), BF),
            pltpu.VMEM((3, SEQ, 256), F32),
            pltpu.VMEM((32, 16, 384), BF),
            pltpu.VMEM((32, 16, 384), BF),
            pltpu.VMEM((3, 4, TOK, LANES), BF),
            pltpu.VMEM((SEQ, 1024), BF),
            pltpu.VMEM((3, TOK, 1024), BF),
            pltpu.VMEM((CHUNKS, SEQ // CHUNKS, 1024), BF),
            pltpu.VMEM((CHUNKS, SEQ // CHUNKS, 1024), BF),
            dma((5,)),
            dma((5, 2, 4)),
            dma((5, 2, 4)),
            dma((7,)),
            dma((7,)),
            dma((3, 3, 2)),
            dma((3, 3, 2)),
            dma((3, 4, 2)),
            dma((3, NX, 2)),
            dma((7, CHUNKS)),
            dma((7, CHUNKS)),
            dma((3, NX, 4)),
            dma((3, NX, 4)),
            dma((5, 2)),
            dma((5, 2)),
            dma((5, 2)),
            dma((5, 2)),
            dma((7,)),
            dma((7,)),
            dma((31,)),
            dma((31,)),
        ],
        compiler_params=pltpu.CompilerParams(collective_id=0, has_side_effects=True, vmem_limit_bytes=40 << 20),
        name="step",
    )(tile_counts, image_offsets, vis, affine, proj, qkv, text_rows[0],
      attn_gain[None], jnp.asarray(cos), jnp.asarray(sin))
    return out[None]


def solution(mesh):
    in_specs = (
        P(None, "dp", None, "tensor"),
        P(),
        P(),
        P("dp", None, "tensor"),
        P("dp", None, "tensor"),
        P(),
        P("dp", "tensor"),
        P("dp", None, "tensor"),
        P(),
        P("dp"),
    )
    return jax.shard_map(per_device, mesh=mesh, in_specs=in_specs,
                         out_specs=P("dp", None, "tensor"), check_vma=False)
```

time: 142 us -> 134 us (0.944)
  the two profiles are of different devices: /device:TPU:8 before, /device:TPU:17 now
where the time goes in v4:
time: 134 us; the launch traced here: 133 us
  Pallas kernels  126 us (94%)
  local copies, waits for them, and re-layouts  5.32 us (4%)
    pallas_call x1, Pallas kernels, per_device(): pl.pallas_call(kernel, out_shape=jax.ShapeDtypeStruct((SEQ, 512), BF), in...  126 us
    unnamed x21, local copies, waits for them, and re-layouts  4.05 us

profile of v4, /device:TPU:17, one launch (start us, length us, event | category | flops | bytes accessed | tf_op | source)
XLA Modules:
  0.0 133.3 jit_solution(17192205710624632422)
XLA Ops:
  0.0 0.0 copy-start.5
  0.0 0.8 fusion
  0.8 0.1 reshape.26
  0.9 0.2 copy.16
  1.1 0.1 copy.17
  1.2 0.0 copy-done.5
  1.2 0.2 reshape.28
  1.4 0.0 copy-start.6
  1.5 0.9 copy-done.6
  2.4 0.0 copy-start.7
  2.4 0.1 copy.20
  2.5 0.8 copy-done.7
  3.3 0.1 copy.19
  3.5 0.0 copy-start.8
  3.5 0.0 copy-start.3
  3.5 0.2 copy.21
  3.7 0.0 copy-start
  3.7 0.7 copy-done.8
  4.4 0.1 reshape.24
  4.5 0.2 copy.14
  4.7 0.0 copy-start.2
  4.7 0.1 copy.15
  4.9 0.0 copy-start.1
  5.6 0.0 copy-start.4
  5.6 0.0 copy-done.3
  5.6 0.0 copy-done
  5.6 0.0 copy-done.2
  5.7 0.2 copy-done.1
  5.8 0.5 copy-done.4
  6.3 126.3 %step.1 = bf16[384,512]{1,0:T(8,128)(2,1)S(1)} custom-call(s32[32]{0:T(128)S(1)} %copy-done.4, s32[1]{0:T(128)S(6)} %copy.26.off_ref, bf16[4,64,256]{2,1,0:T(8,128)(2,1)S(1)} %pad.12.vis_ref, f32[2,4,1,256]{3,2,1,0:T(1,128)S(1)} %pad.13.affine_ref, bf16[2,208,512]{2,1,0:T(8,128)(2,1)S(1)} %bitcast.20, bf16[3,256,256]{2,1,0:T(8,128)(2,1)S(1)} %bitcast.21, ...), custom_call_target="tpu_custom_call" | custom-call | tf_op jit(solution)/shard_map/step/pallas_call | solution.py:620
  132.6 0.7 copy.27
  (5 shorter events, 0.1 us)
Async XLA Ops:
  0.0 1.2 copy-start.5
  1.4 1.0 copy-start.6
  2.4 0.9 copy-start.7
  3.5 0.9 copy-start.8
  3.5 2.1 %copy-start.3 = (f32[8192]{0:T(1024)S(1)}, f32[8192]{0:T(1024)}, u32[]{:S(2)}) copy-start(f32[8192]{0:T(1024)} %param.17) | copy-start | bytes 98308
  3.7 2.0 %copy-start = (bf16[1,384,1024]{2,1,0:T(8,128)(2,1)S(1)}, bf16[1,384,1024]{2,1,0:T(8,128)(2,1)}, u32[]{:S(2)}) copy-start(bf16[1,384,1024]{2,1,0:T(8,128)(2,1)} %param.16) | copy-start | bytes 2359300
  4.7 1.0 copy-start.2
  4.9 1.0 copy-start.1
  5.6 0.7 copy-start.4

commit v5 on v4

--- a/solution.py
+++ b/solution.py
@@ -16,6 +16,9 @@
 SEQ = 384
 TOK = 64
 CHUNKS = 4
+ROW_FOR = ((0, 2, 3, 1), (1, 3, 2, 0), (3, 0, 1, 2), (2, 1, 0, 3))
+COLUMN_FOR = tuple(tuple(row.index(r) for r in range(4)) for row in ROW_FOR)
+SAMPLE_AT = tuple(tuple([row[k] for row in ROW_FOR].index(r) for r in range(4)) for k in range(4))
 NX, NY, NZ = 4, 4, 8
 LANES = 256
 ROWS = 208
@@ -45,7 +48,7 @@
     out_ref,
     wp, wq, vis_all, vis_own, stats, image_stats, text_ref, pick_ref, sel_ref, acts, vs, im, ia,
     v_fo, v_fi, v_no, v_ni, v_own, i_fo, i_fi, i_no, i_ni, i_own, t_fo, t_fi, t_no, t_ni, t_own,
-    a2s, a2r, vis_col, text_mid, im_col, relay_y, relay_x,
+    a2s, a2r, vis_col, text_mid, im_col,
     l_sem, z_s, z_r, st_s, st_r, ys_s, ys_r, xs_s, xs_r, tx_s, tx_r, d_s, d_r, f_s, f_r, g_s, g_r, n_s, n_r,
     a_s, a_r,
 ):
@@ -169,71 +172,51 @@
         lambda j, h: vis_col.at[j, pl.ds(2 * h, 2)],
         lambda core, s, h: vis_all.at[pl.ds(4 * core + 2 * h, 2), s],
     )
-    def crossed(a, b):
-        return ((a // 2 + b // 2) % 2) * 2 + (a + b) % 2
+    def entry(rows, a, b):
+        value = jnp.int32(0)
+        for i, row in enumerate(rows):
+            for j, v in enumerate(row):
+                value = value + jnp.where((a == i) & (b == j), v, 0)
+        return value
 
     class TextSpread:
+        def __init__(self):
+            self.row = entry(ROW_FOR, x, y)
+            self.column = entry(COLUMN_FOR, x, y)
+            self.sample = {step: entry(SAMPLE_AT, x, (y + step + NY) % NY) for step in (0, -1, 1, 2)}
+
         def part(self, q):
             return pl.ds(q * (SEQ // CHUNKS), SEQ // CHUNKS)
 
         def block(self, core, step, q):
-            return acts.at[core, crossed(x, (y + step + NY) % NY), self.part(q)]
-
-        def hop(self, q, at, src, dst, relay, kind, along):
-            other = x if along == "y" else y
-
-            def device(place):
-                return (dp, place * 2 + c) if along == "y" else (place * NZ + z, tn)
-
+            return acts.at[core, self.sample[step], self.part(q)]
+
+        def hop(self, q, stays, src, dst, kind, to):
             ssem, rsem = tx_s.at[kind, q], tx_r.at[kind, q]
-            straight = remote(src, dst, ssem, rsem, device(crossed(at, other)))
+            copy = remote(src, dst, ssem, rsem, to)
             local = pltpu.make_async_copy(src, dst, rsem)
-            beside = device((at + (1 if q % 2 == 0 else 3)) % 4)
-            via = remote(src, relay.at[q], ssem, tx_r.at[kind + 1, q], beside)
-
-            @pl.when(other == 0)
+
+            @pl.when(stays)
             def _():
                 local.start()
 
-            @pl.when((other == 1) | (other == 3))
+            @pl.when(jnp.logical_not(stays))
             def _():
-                straight.start()
-
-            @pl.when(other == 2)
-            def _():
-                via.start()
-
-            later.append((straight, other != 0))
-
-        def relay(self, q, at, dst, relay, kind, along):
-            other = x if along == "y" else y
-            nxt = (at + (1 if q % 2 == 0 else 3)) % 4
-            to = (dp, nxt * 2 + c) if along == "y" else (nxt * NZ + z, tn)
-            on = remote(relay.at[q], dst, tx_s.at[kind + 1, q], tx_r.at[kind, q], to)
-
-            @pl.when(other == 2)
-            def _():
-                remote(relay.at[q], relay.at[q], tx_s.at[kind + 1, q], tx_r.at[kind + 1, q],
-                       here).wait_recv()
-                on.start()
-
-            later.append((on, other == 2))
+                copy.start()
+
+            later.append((copy, jnp.logical_not(stays)))
 
         def begin(self):
             for q in range(CHUNKS):
-                self.hop(q, y, text_ref.at[self.part(q)], text_mid.at[self.part(q)], relay_y, 0, "y")
-
-        def pass_y(self, q):
-            self.relay(q, y, text_mid.at[self.part(q)], relay_y, 0, "y")
+                part = self.part(q)
+                self.hop(q, self.row == y, text_ref.at[part], text_mid.at[part], 0,
+                         (dp, self.row * 2 + c))
 
         def turn(self, q):
             mid = text_mid.at[self.part(q)]
             arrived(mid, tx_s.at[0, q], tx_r.at[0, q])
-            self.hop(q, x, mid, acts.at[c, x, self.part(q)], relay_x, 2, "x")
-
-        def pass_x(self, q):
-            source = (x + (3 if q % 2 == 0 else 1)) % NX
-            self.relay(q, x, acts.at[c, source, self.part(q)], relay_x, 2, "x")
+            self.hop(q, self.column == x, mid, acts.at[c, x, self.part(q)], 2,
+                     (self.column * NZ + z, tn))
 
         def on_y(self, q, block_step, step, kind):
             ref = self.block(c, block_step, q)
@@ -458,60 +441,52 @@
     vis_spread.near(0)
     vis_spread.near(1)
     ring(1)
-    text_spread.pass_y(0)
-    text_spread.pass_y(1)
     text_spread.turn(0)
     text_spread.turn(1)
     ring(2)
-    text_spread.pass_y(2)
-    text_spread.pass_y(3)
     text_spread.turn(2)
     text_spread.turn(3)
     vis_spread.far(0)
     vis_spread.far(1)
-    text_spread.pass_x(0)
-    text_spread.pass_x(1)
     text_spread.mine(0)
     text_spread.mine(1)
     ring(3)
-    text_spread.pass_x(2)
-    text_spread.pass_x(3)
     text_spread.mine(2)
     text_spread.mine(3)
     vis_spread.to_sibling()
     text_spread.near(0)
+    text_spread.near(1)
     ring(4)
     locals_done((0, 1))
     vision()
     vis_reduce.opposite()
-    text_spread.near(1)
     text_spread.near(2)
+    text_spread.near(3)
     vis_reduce.neighbours()
-    text_spread.near(3)
-    ring(5)
     text_spread.far(0)
     text_spread.far(1)
+    ring(5)
     image()
-    ring(6)
     text_spread.far(2)
     text_spread.far(3)
     image_spread.near(0)
     image_spread.near(1)
+    ring(6)
+    image_spread.far(0)
+    image_spread.far(1)
     text_spread.from_sibling()
     locals_done((2, 3, 4))
     text_reduce[0].opposite()
     ring(7)
-    image_spread.far(0)
-    image_spread.far(1)
+    image_spread.to_sibling()
     text_reduce[1].opposite()
     text_reduce[0].neighbours()
+    image_spread.from_sibling()
     ring(8)
-    image_spread.to_sibling()
+    image_reduce.opposite()
+    image_reduce.neighbours()
     text_reduce[2].opposite()
-    image_spread.from_sibling()
-    image_reduce.opposite()
     text_reduce[1].neighbours()
-    image_reduce.neighbours()
     text_reduce[2].neighbours()
 
     total = image_stats[tn]
@@ -656,8 +631,6 @@
             pltpu.VMEM((3, 4, TOK, LANES), BF),
             pltpu.VMEM((SEQ, 1024), BF),
             pltpu.VMEM((3, TOK, 1024), BF),
-            pltpu.VMEM((CHUNKS, SEQ // CHUNKS, 1024), BF),
-            pltpu.VMEM((CHUNKS, SEQ // CHUNKS, 1024), BF),
             dma((5,)),
             dma((5, 2, 4)),
             dma((5, 2, 4)),

time: 134 us -> 122 us (0.910)
  the two profiles are of different devices: /device:TPU:17 before, /device:TPU:8 now
where the time goes in v5:
time: 122 us; the launch traced here: 121 us
  Pallas kernels  114 us (93%)
  local copies, waits for them, and re-layouts  5.32 us (4%)
    pallas_call x1, Pallas kernels, per_device(): pl.pallas_call(kernel, out_shape=jax.ShapeDtypeStruct((SEQ, 512), BF), in...  114 us
    unnamed x21, local copies, waits for them, and re-layouts  4.05 us

profile of v5, /device:TPU:8, one launch (start us, length us, event | category | flops | bytes accessed | tf_op | source)
XLA Modules:
  0.0 121.2 jit_solution(2411363348975848656)
XLA Ops:
  0.0 0.0 copy-start.5
  0.0 0.8 fusion
  0.8 0.1 reshape.26
  0.9 0.2 copy.16
  1.1 0.1 copy.17
  1.2 0.0 copy-done.5
  1.2 0.2 reshape.28
  1.4 0.0 copy-start.6
  1.5 0.9 copy-done.6
  2.4 0.0 copy-start.7
  2.4 0.1 copy.20
  2.5 0.8 copy-done.7
  3.3 0.1 copy.19
  3.5 0.0 copy-start.8
  3.5 0.0 copy-start.3
  3.5 0.2 copy.21
  3.7 0.0 copy-start
  3.7 0.7 copy-done.8
  4.4 0.1 reshape.24
  4.5 0.2 copy.14
  4.7 0.0 copy-start.2
  4.7 0.1 copy.15
  4.9 0.0 copy-start.1
  5.6 0.0 copy-start.4
  5.6 0.0 copy-done.3
  5.6 0.0 copy-done
  5.6 0.0 copy-done.2
  5.7 0.2 copy-done.1
  5.8 0.5 copy-done.4
  6.3 114.2 %step.1 = bf16[384,512]{1,0:T(8,128)(2,1)S(1)} custom-call(s32[32]{0:T(128)S(1)} %copy-done.4, s32[1]{0:T(128)S(6)} %copy.26.off_ref, bf16[4,64,256]{2,1,0:T(8,128)(2,1)S(1)} %pad.12.vis_ref, f32[2,4,1,256]{3,2,1,0:T(1,128)S(1)} %pad.13.affine_ref, bf16[2,208,512]{2,1,0:T(8,128)(2,1)S(1)} %bitcast.20, bf16[3,256,256]{2,1,0:T(8,128)(2,1)S(1)} %bitcast.21, ...), custom_call_target="tpu_custom_call" | custom-call | tf_op jit(solution)/shard_map/step/pallas_call | solution.py:595
  120.5 0.7 copy.27
  (5 shorter events, 0.1 us)
Async XLA Ops:
  0.0 1.2 %copy-start.5 = (bf16[100,2,1024]{2,1,0:T(2,128)(2,1)S(1)}, bf16[100,2,1024]{2,1,0:T(2,128)(2,1)}, u32[]{:S(2)}) copy-start(bf16[100,2,1024]{2,1,0:T(2,128)(2,1)} %param.15) | copy-start | bytes 1228804
  1.4 1.0 copy-start.6
  2.4 0.9 copy-start.7
  3.5 0.9 copy-start.8
  3.5 2.1 %copy-start.3 = (f32[8192]{0:T(1024)S(1)}, f32[8192]{0:T(1024)}, u32[]{:S(2)}) copy-start(f32[8192]{0:T(1024)} %param.17) | copy-start | bytes 98308
  3.7 2.0 %copy-start = (bf16[1,384,1024]{2,1,0:T(8,128)(2,1)S(1)}, bf16[1,384,1024]{2,1,0:T(8,128)(2,1)}, u32[]{:S(2)}) copy-start(bf16[1,384,1024]{2,1,0:T(8,128)(2,1)} %param.16) | copy-start | bytes 2359300
  4.7 1.0 copy-start.2
  4.9 1.0 copy-start.1
  5.6 0.7 copy-start.4

commit v6 on v5

--- a/solution.py
+++ b/solution.py
@@ -44,11 +44,11 @@
 
 
 def kernel(
-    cnt_ref, off_ref, vis_ref, affine_ref, proj_ref, qkv_ref, raw_ref, attn_ref, cos_ref, sin_ref,
+    cnt_ref, off_ref, vis_ref, affine_ref, proj_ref, query_ref, keyval_ref, raw_ref, attn_ref, cos_ref, sin_ref,
     out_ref,
     wp, wq, vis_all, vis_own, stats, image_stats, text_ref, pick_ref, sel_ref, acts, vs, im, ia,
-    v_fo, v_fi, v_no, v_ni, v_own, i_fo, i_fi, i_no, i_ni, i_own, t_fo, t_fi, t_no, t_ni, t_own,
-    a2s, a2r, vis_col, text_mid, im_col,
+    v_fo, v_fi, v_no, v_ni, v_own, i_fo, i_fi, i_no, i_ni, i_own, j_fo, j_fi, j_no, j_ni, j_own, t_fo, t_fi, t_no, t_ni, t_own,
+    qs, qr, ks, kr, vis_col, text_mid, im_col,
     l_sem, z_s, z_r, st_s, st_r, ys_s, ys_r, xs_s, xs_r, tx_s, tx_r, d_s, d_r, f_s, f_r, g_s, g_r, n_s, n_r,
     a_s, a_r,
 ):
@@ -75,7 +75,9 @@
         remote(ref, ref, ssem, rsem, here).wait_recv()
 
     def own(u):
-        return proj_ref.at[u] if u < 2 else qkv_ref.at[u - 2]
+        if u < 2:
+            return proj_ref.at[u]
+        return keyval_ref if u == 4 else query_ref.at[:, pl.ds(256 * (u - 2), 256)]
 
     def slot_ref(u, source):
         if u < 2:
@@ -404,10 +406,11 @@
         return first + dot(source[1, s], wq[u, 4:8].reshape(1024, 256))
 
     vis_reduce = Reduce(0, v_fo, v_fi, v_no, v_ni, v_own, lambda o: vs[(x + o) % NX])
-    image_reduce = Reduce(
+    image_queries = Reduce(
         1, i_fo, i_fi, i_no, i_ni, i_own,
-        lambda o: jnp.concatenate([project(ia, u, o) for u in range(3)], axis=1),
+        lambda o: jnp.concatenate([project(ia, u, o) for u in range(2)], axis=1),
     )
+    image_keyvals = Reduce(5, j_fo, j_fi, j_no, j_ni, j_own, lambda o: project(ia, 2, o))
     text_reduce = [
         Reduce(2 + u, t_fo.at[u], t_fi.at[u], t_no.at[u], t_ni.at[u], t_own.at[u],
                lambda o, u=u: project(acts, u, o))
@@ -437,6 +440,46 @@
     def locals_done(us):
         for u in us:
             locals_[u].wait()
+
+    def image_scale():
+        total = image_stats[tn]
+        for o in range(1, 8):
+            source = (tn - o + 8) % 8
+            arrived(image_stats.at[source], n_s.at[o - 1], n_r.at[o - 1])
+            total = total + image_stats[source]
+        return column_of([lax.rsqrt(total[0:1] / 8192.0 + decoder_epsilon)], TOK)
+
+    def route(i, reduced, scale, out, into):
+        half = out.shape[2]
+        rows = (reduced.total() * scale).astype(BF)
+        both = jnp.concatenate([rows[:, 0:half], rows[:, half : 2 * half]], axis=0)
+        out[...] = dot(pick_ref[...], both).astype(BF).reshape(32, 16, half)
+        into[dp] = out[dp]
+
+        def one(o, carry):
+            to = (dp + o) % 32
+            remote(out.at[to], into.at[dp], a_s.at[i, o - 1], a_r.at[i, o - 1], (to, tn)).start()
+            return carry
+
+        lax.fori_loop(1, 32, one, 0)
+
+    def routed(i, out, into):
+        def one(o, carry):
+            source = (dp - o + 32) % 32
+            remote(out.at[source], into.at[source], a_s.at[i, o - 1], a_r.at[i, o - 1],
+                   here).wait_recv()
+            return carry
+
+        lax.fori_loop(1, 32, one, 0)
+        return into[...].reshape(512, into.shape[2])
+
+    def routes_sent(i, out, into):
+        def one(o, carry):
+            to = (dp + o) % 32
+            remote(out.at[to], into.at[dp], a_s.at[i, o - 1], a_r.at[i, o - 1], here).wait_send()
+            return carry
+
+        lax.fori_loop(1, 32, one, 0)
 
     vis_spread.near(0)
     vis_spread.near(1)
@@ -480,53 +523,34 @@
     ring(7)
     image_spread.to_sibling()
     text_reduce[1].opposite()
+    image_spread.from_sibling()
+    image_queries.opposite()
     text_reduce[0].neighbours()
-    image_spread.from_sibling()
     ring(8)
-    image_reduce.opposite()
-    image_reduce.neighbours()
+    image_keyvals.opposite()
+    scale = image_scale()
+    image_queries.neighbours()
     text_reduce[2].opposite()
+    image_keyvals.neighbours()
+    route(0, image_queries, scale, qs, qr)
     text_reduce[1].neighbours()
+    route(1, image_keyvals, scale, ks, kr)
     text_reduce[2].neighbours()
 
-    total = image_stats[tn]
-    for o in range(1, 8):
-        source = (tn - o + 8) % 8
-        arrived(image_stats.at[source], n_s.at[o - 1], n_r.at[o - 1])
-        total = total + image_stats[source]
-    image_scale = column_of([lax.rsqrt(total[0:1] / 8192.0 + decoder_epsilon)], TOK)
-    image_rows = (image_reduce.total() * image_scale).astype(BF)
-    low, high = image_rows[:, 0:384], image_rows[:, 384:768]
-    both = jnp.concatenate([low, high], axis=0)
-    a2s[...] = dot(pick_ref[...], both).astype(BF).reshape(32, 16, 384)
-    a2r[dp] = a2s[dp]
-
-    def route(o, carry):
-        to = (dp + o) % 32
-        remote(a2s.at[to], a2r.at[dp], a_s.at[o - 1], a_r.at[o - 1], (to, tn)).start()
-        return carry
-
-    lax.fori_loop(1, 32, route, 0)
-
     causal = row_of((SEQ, SEQ)) >= lane_of((SEQ, SEQ))
 
-    def route_done(o, carry):
-        source = (dp - o + 32) % 32
-        remote(a2s.at[source], a2r.at[source], a_s.at[o - 1], a_r.at[o - 1], here).wait_recv()
-        return carry
-
-    lax.fori_loop(1, 32, route_done, 0)
-    routed = a2r[...].reshape(512, 384)
-    image_low = dot(sel_ref[0], routed)
-    image_high = dot(sel_ref[1], routed)
+    images_q = routed(0, qs, qr)
+    images_k = routed(1, ks, kr)
+    placed = [dot(sel_ref[h], images) for images in (images_q, images_k) for h in range(2)]
 
     texts = [text_reduce[u].total() for u in range(3)]
     cos, sin = cos_ref[...], sin_ref[...]
 
     def column(i):
         text = texts[i // 2][:, 128 * (i % 2) : 128 * (i % 2) + 128]
-        picture = image_low if i < 3 else image_high
-        picture = picture[:, 128 * (i % 3) : 128 * (i % 3) + 128]
+        picture = placed[i // 2] if i < 4 else placed[i - 2]
+        if i < 4:
+            picture = picture[:, 128 * (i % 2) : 128 * (i % 2) + 128]
         return jnp.where(is_image, picture, text)
 
     def turned(value):
@@ -551,12 +575,8 @@
             copy.wait_send()
 
 
-    def sent(o, carry):
-        to = (dp + o) % 32
-        remote(a2s.at[to], a2r.at[dp], a_s.at[o - 1], a_r.at[o - 1], here).wait_send()
-        return carry
-
-    lax.fori_loop(1, 32, sent, 0)
+    routes_sent(0, qs, qr)
+    routes_sent(1, ks, kr)
 
 
 def rotation_tables():
@@ -586,8 +606,6 @@
 
     proj = jnp.pad(proj_weight.reshape(PART, 1024), ((0, ROWS - PART), (0, 0)))
     proj = proj.reshape(ROWS, 2, 512).transpose(1, 0, 2)
-    qkv = jnp.concatenate([w_query, key_value_weight.reshape(256, 256)], axis=1)
-    qkv = qkv.reshape(256, 3, 256).transpose(1, 0, 2)
     cos, sin = rotation_tables()
     vmem = pl.BlockSpec(memory_space=pltpu.VMEM)
     smem = pl.BlockSpec(memory_space=pltpu.SMEM)
@@ -595,7 +613,7 @@
     out = pl.pallas_call(
         kernel,
         out_shape=jax.ShapeDtypeStruct((SEQ, 512), BF),
-        in_specs=[smem, smem] + [vmem] * 8,
+        in_specs=[smem, smem] + [vmem] * 9,
         out_specs=vmem,
         scratch_shapes=[
             pltpu.VMEM((2, NZ, LANES, 512), BF),
@@ -616,18 +634,25 @@
             pltpu.VMEM((2, TOK, 1024), BF),
             pltpu.VMEM((2, TOK, 1024), BF),
             pltpu.VMEM((TOK, 1024), F32),
-            pltpu.VMEM((TOK, 768), BF),
-            pltpu.VMEM((TOK, 768), BF),
-            pltpu.VMEM((2, TOK, 768), BF),
-            pltpu.VMEM((2, TOK, 768), BF),
-            pltpu.VMEM((TOK, 768), F32),
+            pltpu.VMEM((TOK, 512), BF),
+            pltpu.VMEM((TOK, 512), BF),
+            pltpu.VMEM((2, TOK, 512), BF),
+            pltpu.VMEM((2, TOK, 512), BF),
+            pltpu.VMEM((TOK, 512), F32),
+            pltpu.VMEM((TOK, 256), BF),
+            pltpu.VMEM((TOK, 256), BF),
+            pltpu.VMEM((2, TOK, 256), BF),
+            pltpu.VMEM((2, TOK, 256), BF),
+            pltpu.VMEM((TOK, 256), F32),
             pltpu.VMEM((3, SEQ, 256), BF),
             pltpu.VMEM((3, SEQ, 256), BF),
             pltpu.VMEM((3, 2, SEQ, 256), BF),
             pltpu.VMEM((3, 2, SEQ, 256), BF),
             pltpu.VMEM((3, SEQ, 256), F32),
-            pltpu.VMEM((32, 16, 384), BF),
-            pltpu.VMEM((32, 16, 384), BF),
+            pltpu.VMEM((32, 16, 256), BF),
+            pltpu.VMEM((32, 16, 256), BF),
+            pltpu.VMEM((32, 16, 128), BF),
+            pltpu.VMEM((32, 16, 128), BF),
             pltpu.VMEM((3, 4, TOK, LANES), BF),
             pltpu.VMEM((SEQ, 1024), BF),
             pltpu.VMEM((3, TOK, 1024), BF),
@@ -644,18 +669,19 @@
             dma((7, CHUNKS)),
             dma((3, NX, 4)),
             dma((3, NX, 4)),
-            dma((5, 2)),
-            dma((5, 2)),
-            dma((5, 2)),
-            dma((5, 2)),
+            dma((6, 2)),
+            dma((6, 2)),
+            dma((6, 2)),
+            dma((6, 2)),
             dma((7,)),
             dma((7,)),
-            dma((31,)),
-            dma((31,)),
+            dma((2, 31)),
+            dma((2, 31)),
         ],
         compiler_params=pltpu.CompilerParams(collective_id=0, has_side_effects=True, vmem_limit_bytes=40 << 20),
         name="step",
-    )(tile_counts, image_offsets, vis, affine, proj, qkv, text_rows[0],
+    )(tile_counts, image_offsets, vis, affine, proj, w_query,
+      key_value_weight.reshape(256, 256), text_rows[0],
       attn_gain[None], jnp.asarray(cos), jnp.asarray(sin))
     return out[None]
 

time: 122 us -> 119 us (0.975)
  local copies, waits for them, and re-layouts: 5.32 us -> 3.39 us
    unnamed x21 -> x20, local copies, waits for them, and re-layouts: 4.05 us -> 2.29 us
where the time goes in v6:
time: 119 us
  Pallas kernels  114 us (96%)
  local copies, waits for them, and re-layouts  3.39 us (3%)
    pallas_call x1, Pallas kernels, per_device(): pl.pallas_call(kernel, out_shape=jax.ShapeDtypeStruct((SEQ, 512), BF), in...  114 us

profile of v6, /device:TPU:8, one launch (start us, length us, event | category | flops | bytes accessed | tf_op | source)
XLA Modules:
  0.0 119.3 jit_solution(5785824641980430421)
XLA Ops:
  0.0 0.0 copy-start.6
  0.0 0.8 fusion
  0.8 0.1 reshape.23
  0.9 0.2 copy.16
  1.1 0.1 copy.17
  1.2 0.0 copy-done.6
  1.2 0.2 reshape.25
  1.4 0.0 copy-start.7
  1.5 0.0 copy-start.8
  1.5 0.0 copy-start.4
  1.5 0.0 copy-start
  1.5 0.8 copy-done.7
  2.4 0.1 reshape.21
  2.5 0.2 copy.14
  2.7 0.0 copy-start.3
  2.7 0.1 copy.15
  2.9 0.0 copy-start.1
  2.9 0.0 copy-start.2
  2.9 0.0 copy-done.8
  3.7 0.0 copy-start.5
  3.7 0.0 copy-done.4
  3.7 0.0 copy-done
  3.7 0.0 copy-done.3
  3.7 0.1 copy-done.1
  3.8 0.1 copy-done.2
  3.9 0.5 copy-done.5
  4.4 114.1 %step.1 = bf16[384,512]{1,0:T(8,128)(2,1)S(1)} custom-call(s32[32]{0:T(128)S(1)} %copy-done.5, s32[1]{0:T(128)S(6)} %copy.26.off_ref, bf16[4,64,256]{2,1,0:T(8,128)(2,1)S(1)} %pad.12.vis_ref, f32[2,4,1,256]{3,2,1,0:T(1,128)S(1)} %pad.13.affine_ref, bf16[2,208,512]{2,1,0:T(8,128)(2,1)S(1)} %bitcast.21, bf16[256,512]{1,0:T(8,128)(2,1)S(1)} %copy-done.1, ...), custom_call_target="tpu_custom_call" | custom-call | tf_op jit(solution)/shard_map/step/pallas_call | solution.py:613
  118.5 0.7 copy.27
  (5 shorter events, 0.1 us)
Async XLA Ops:
  0.0 1.2 %copy-start.6 = (bf16[100,2,1024]{2,1,0:T(2,128)(2,1)S(1)}, bf16[100,2,1024]{2,1,0:T(2,128)(2,1)}, u32[]{:S(2)}) copy-start(bf16[100,2,1024]{2,1,0:T(2,128)(2,1)} %param.15) | copy-start | bytes 1228804
  1.4 0.9 copy-start.7
  1.5 1.4 %copy-start.8 = (bf16[256,2,128]{2,1,0:T(2,128)(2,1)S(1)}, bf16[256,2,128]{2,1,0:T(2,128)(2,1)}, u32[]{:S(2)}) copy-start(bf16[256,2,128]{2,1,0:T(2,128)(2,1)} %param.19) | copy-start | bytes 393220
  1.5 2.2 %copy-start.4 = (f32[8192]{0:T(1024)S(1)}, f32[8192]{0:T(1024)}, u32[]{:S(2)}) copy-start(f32[8192]{0:T(1024)} %param.17) | copy-start | bytes 98308
  1.5 2.2 %copy-start = (bf16[1,384,1024]{2,1,0:T(8,128)(2,1)S(1)}, bf16[1,384,1024]{2,1,0:T(8,128)(2,1)}, u32[]{:S(2)}) copy-start(bf16[1,384,1024]{2,1,0:T(8,128)(2,1)} %param.16) | copy-start | bytes 2359300
  2.7 1.0 copy-start.3
  2.9 1.0 copy-start.1
  2.9 1.0 copy-start.2
  3.7 0.7 copy-start.5

commit v7 on v6

--- a/solution.py
+++ b/solution.py
@@ -48,7 +48,7 @@
     out_ref,
     wp, wq, vis_all, vis_own, stats, image_stats, text_ref, pick_ref, sel_ref, acts, vs, im, ia,
     v_fo, v_fi, v_no, v_ni, v_own, i_fo, i_fi, i_no, i_ni, i_own, j_fo, j_fi, j_no, j_ni, j_own, t_fo, t_fi, t_no, t_ni, t_own,
-    qs, qr, ks, kr, vis_col, text_mid, im_col,
+    pair_ref, qs, qr, ks, kr, vis_col, text_mid, im_col,
     l_sem, z_s, z_r, st_s, st_r, ys_s, ys_r, xs_s, xs_r, tx_s, tx_r, d_s, d_r, f_s, f_r, g_s, g_r, n_s, n_r,
     a_s, a_r,
 ):
@@ -364,28 +364,33 @@
     text_spread.begin()
 
     class Reduce:
-        def __init__(self, index, far_out, far_in, near_out, near_in, own, value):
-            self.i, self.value, self.own = index, value, own
+        def __init__(self, index, far_out, far_in, near_out, near_in, own, value, both=None):
+            self.i, self.value, self.own, self.both = index, value, own, both
             self.far_out, self.far_in = far_out, far_in
             self.near_out, self.near_in = near_out, near_in
             self.half = far_out.shape[0] // 2
 
         def opposite(self):
             i, half = self.i, self.half
-            self.far_out[...] = self.value(2).astype(BF)
+            if self.both is not None:
+                self.both(2, 0)
+            opposite = self.value(2) if self.both is None else pair_ref[0]
+            self.far_out[...] = opposite.astype(BF)
             for h in range(2):
                 part = pl.ds(half * h, half)
                 send(self.far_out.at[part], self.far_in.at[part], f_s.at[i, h], f_r.at[i, h],
                      along_x(1 if h == 0 else 3))
-            self.own[...] = self.value(0)
+            self.own[...] = self.value(0) if self.both is None else pair_ref[1]
 
         def neighbours(self):
             i, half = self.i, self.half
+            if self.both is not None:
+                self.both(1, 3)
             for h in range(2):
                 part = pl.ds(half * h, half)
                 rest = pl.ds(half * (1 - h), half)
                 o = 1 if h == 0 else 3
-                value = self.value(o)
+                value = self.value(o) if self.both is None else pair_ref[h]
                 arrived(self.far_in.at[part], f_s.at[i, h], f_r.at[i, h])
                 mine = value[half * h : half * h + half] + self.far_in[part, :].astype(F32)
                 self.near_out[h, part, :] = mine.astype(BF)
@@ -401,9 +406,16 @@
             return acc
 
     def project(source, u, o):
-        s = (x + o) % NX
+        s = (x + o + NX) % NX
         first = dot(source[0, s], wq[u, 0:4].reshape(1024, 256))
         return first + dot(source[1, s], wq[u, 4:8].reshape(1024, 256))
+
+    def text_pair(u, a, b):
+        def one(i, carry):
+            pair_ref[i] = project(acts, u, a + i * (b - a))
+            return carry
+
+        lax.fori_loop(0, 2, one, 0)
 
     vis_reduce = Reduce(0, v_fo, v_fi, v_no, v_ni, v_own, lambda o: vs[(x + o) % NX])
     image_queries = Reduce(
@@ -413,7 +425,7 @@
     image_keyvals = Reduce(5, j_fo, j_fi, j_no, j_ni, j_own, lambda o: project(ia, 2, o))
     text_reduce = [
         Reduce(2 + u, t_fo.at[u], t_fi.at[u], t_no.at[u], t_ni.at[u], t_own.at[u],
-               lambda o, u=u: project(acts, u, o))
+               None, functools.partial(text_pair, u))
         for u in range(3)
     ]
 
@@ -504,8 +516,8 @@
     vision()
     vis_reduce.opposite()
     text_spread.near(2)
+    vis_reduce.neighbours()
     text_spread.near(3)
-    vis_reduce.neighbours()
     text_spread.far(0)
     text_spread.far(1)
     ring(5)
@@ -520,20 +532,20 @@
     text_spread.from_sibling()
     locals_done((2, 3, 4))
     text_reduce[0].opposite()
+    image_spread.to_sibling()
     ring(7)
-    image_spread.to_sibling()
     text_reduce[1].opposite()
+    text_reduce[0].neighbours()
     image_spread.from_sibling()
     image_queries.opposite()
-    text_reduce[0].neighbours()
     ring(8)
     image_keyvals.opposite()
+    text_reduce[2].opposite()
     scale = image_scale()
     image_queries.neighbours()
-    text_reduce[2].opposite()
     image_keyvals.neighbours()
+    text_reduce[1].neighbours()
     route(0, image_queries, scale, qs, qr)
-    text_reduce[1].neighbours()
     route(1, image_keyvals, scale, ks, kr)
     text_reduce[2].neighbours()
 
@@ -649,6 +661,7 @@
             pltpu.VMEM((3, 2, SEQ, 256), BF),
             pltpu.VMEM((3, 2, SEQ, 256), BF),
             pltpu.VMEM((3, SEQ, 256), F32),
+            pltpu.VMEM((2, SEQ, 256), F32),
             pltpu.VMEM((32, 16, 256), BF),
             pltpu.VMEM((32, 16, 256), BF),
             pltpu.VMEM((32, 16, 128), BF),

time: 119 us -> 117 us (0.983)
  Pallas kernels: 114 us -> 112 us
    pallas_call x1, Pallas kernels: 114 us -> 112 us  [per_device(): pl.pallas_call(kernel, out_shape=jax.ShapeDtypeStruct((SEQ, 512), BF), in...]
where the time goes in v7:
time: 117 us
  Pallas kernels  112 us (96%)
  local copies, waits for them, and re-layouts  3.39 us (3%)
    pallas_call x1, Pallas kernels, per_device(): pl.pallas_call(kernel, out_shape=jax.ShapeDtypeStruct((SEQ, 512), BF), in...  112 us

profile of v7, /device:TPU:8, one launch (start us, length us, event | category | flops | bytes accessed | tf_op | source)
XLA Modules:
  0.0 117.3 jit_solution(17252997027261164736)
XLA Ops:
  0.0 0.0 copy-start.6
  0.0 0.8 fusion
  0.8 0.1 reshape.23
  0.9 0.2 copy.16
  1.1 0.1 copy.17
  1.2 0.0 copy-done.6
  1.2 0.2 reshape.25
  1.4 0.0 copy-start.7
  1.5 0.0 copy-start.8
  1.5 0.0 copy-start.4
  1.5 0.0 copy-start
  1.5 0.8 copy-done.7
  2.4 0.1 reshape.21
  2.5 0.2 copy.14
  2.7 0.0 copy-start.3
  2.7 0.1 copy.15
  2.9 0.0 copy-start.1
  2.9 0.0 copy-start.2
  2.9 0.0 copy-done.8
  3.7 0.0 copy-start.5
  3.7 0.0 copy-done.4
  3.7 0.0 copy-done
  3.7 0.0 copy-done.3
  3.7 0.1 copy-done.1
  3.8 0.1 copy-done.2
  3.9 0.5 copy-done.5
  4.4 112.2 %step.1 = bf16[384,512]{1,0:T(8,128)(2,1)S(1)} custom-call(s32[32]{0:T(128)S(1)} %copy-done.5, s32[1]{0:T(128)S(6)} %copy.26.off_ref, bf16[4,64,256]{2,1,0:T(8,128)(2,1)S(1)} %pad.12.vis_ref, f32[2,4,1,256]{3,2,1,0:T(1,128)S(1)} %pad.13.affine_ref, bf16[2,208,512]{2,1,0:T(8,128)(2,1)S(1)} %bitcast.21, bf16[256,512]{1,0:T(8,128)(2,1)S(1)} %copy-done.1, ...), custom_call_target="tpu_custom_call" | custom-call | tf_op jit(solution)/shard_map/step/pallas_call | solution.py:625
  116.6 0.7 copy.27
  (5 shorter events, 0.1 us)
Async XLA Ops:
  0.0 1.2 %copy-start.6 = (bf16[100,2,1024]{2,1,0:T(2,128)(2,1)S(1)}, bf16[100,2,1024]{2,1,0:T(2,128)(2,1)}, u32[]{:S(2)}) copy-start(bf16[100,2,1024]{2,1,0:T(2,128)(2,1)} %param.15) | copy-start | bytes 1228804
  1.4 0.9 copy-start.7
  1.5 1.4 %copy-start.8 = (bf16[256,2,128]{2,1,0:T(2,128)(2,1)S(1)}, bf16[256,2,128]{2,1,0:T(2,128)(2,1)}, u32[]{:S(2)}) copy-start(bf16[256,2,128]{2,1,0:T(2,128)(2,1)} %param.19) | copy-start | bytes 393220
  1.5 2.2 %copy-start.4 = (f32[8192]{0:T(1024)S(1)}, f32[8192]{0:T(1024)}, u32[]{:S(2)}) copy-start(f32[8192]{0:T(1024)} %param.17) | copy-start | bytes 98308
  1.5 2.2 %copy-start = (bf16[1,384,1024]{2,1,0:T(8,128)(2,1)S(1)}, bf16[1,384,1024]{2,1,0:T(8,128)(2,1)}, u32[]{:S(2)}) copy-start(bf16[1,384,1024]{2,1,0:T(8,128)(2,1)} %param.16) | copy-start | bytes 2359300
  2.7 1.0 copy-start.3
  2.9 1.0 copy-start.1
  2.9 1.0 copy-start.2
  3.7 0.7 copy-start.5

commit v8 on v7

--- a/solution.py
+++ b/solution.py
@@ -48,7 +48,7 @@
     out_ref,
     wp, wq, vis_all, vis_own, stats, image_stats, text_ref, pick_ref, sel_ref, acts, vs, im, ia,
     v_fo, v_fi, v_no, v_ni, v_own, i_fo, i_fi, i_no, i_ni, i_own, j_fo, j_fi, j_no, j_ni, j_own, t_fo, t_fi, t_no, t_ni, t_own,
-    pair_ref, qs, qr, ks, kr, vis_col, text_mid, im_col,
+    pair_ref, qpair_ref, kpair_ref, qs, qr, ks, kr, vis_col, text_mid, im_col,
     l_sem, z_s, z_r, st_s, st_r, ys_s, ys_r, xs_s, xs_r, tx_s, tx_r, d_s, d_r, f_s, f_r, g_s, g_r, n_s, n_r,
     a_s, a_r,
 ):
@@ -364,8 +364,8 @@
     text_spread.begin()
 
     class Reduce:
-        def __init__(self, index, far_out, far_in, near_out, near_in, own, value, both=None):
-            self.i, self.value, self.own, self.both = index, value, own, both
+        def __init__(self, index, far_out, far_in, near_out, near_in, own, value, both=None, pair=None):
+            self.i, self.value, self.own, self.both, self.pair = index, value, own, both, pair
             self.far_out, self.far_in = far_out, far_in
             self.near_out, self.near_in = near_out, near_in
             self.half = far_out.shape[0] // 2
@@ -374,13 +374,13 @@
             i, half = self.i, self.half
             if self.both is not None:
                 self.both(2, 0)
-            opposite = self.value(2) if self.both is None else pair_ref[0]
+            opposite = self.value(2) if self.both is None else self.pair[0]
             self.far_out[...] = opposite.astype(BF)
             for h in range(2):
                 part = pl.ds(half * h, half)
                 send(self.far_out.at[part], self.far_in.at[part], f_s.at[i, h], f_r.at[i, h],
                      along_x(1 if h == 0 else 3))
-            self.own[...] = self.value(0) if self.both is None else pair_ref[1]
+            self.own[...] = self.value(0) if self.both is None else self.pair[1]
 
         def neighbours(self):
             i, half = self.i, self.half
@@ -390,7 +390,7 @@
                 part = pl.ds(half * h, half)
                 rest = pl.ds(half * (1 - h), half)
                 o = 1 if h == 0 else 3
-                value = self.value(o) if self.both is None else pair_ref[h]
+                value = self.value(o) if self.both is None else self.pair[h]
                 arrived(self.far_in.at[part], f_s.at[i, h], f_r.at[i, h])
                 mine = value[half * h : half * h + half] + self.far_in[part, :].astype(F32)
                 self.near_out[h, part, :] = mine.astype(BF)
@@ -417,15 +417,22 @@
 
         lax.fori_loop(0, 2, one, 0)
 
+    def image_pair(units, pair, a, b):
+        def one(i, carry):
+            for n, u in enumerate(units):
+                pair[i, :, 256 * n : 256 * n + 256] = project(ia, u, a + i * (b - a))
+            return carry
+
+        lax.fori_loop(0, 2, one, 0)
+
     vis_reduce = Reduce(0, v_fo, v_fi, v_no, v_ni, v_own, lambda o: vs[(x + o) % NX])
-    image_queries = Reduce(
-        1, i_fo, i_fi, i_no, i_ni, i_own,
-        lambda o: jnp.concatenate([project(ia, u, o) for u in range(2)], axis=1),
-    )
-    image_keyvals = Reduce(5, j_fo, j_fi, j_no, j_ni, j_own, lambda o: project(ia, 2, o))
+    image_queries = Reduce(1, i_fo, i_fi, i_no, i_ni, i_own, None,
+                           functools.partial(image_pair, (0, 1), qpair_ref), qpair_ref)
+    image_keyvals = Reduce(5, j_fo, j_fi, j_no, j_ni, j_own, None,
+                           functools.partial(image_pair, (2,), kpair_ref), kpair_ref)
     text_reduce = [
         Reduce(2 + u, t_fo.at[u], t_fi.at[u], t_no.at[u], t_ni.at[u], t_own.at[u],
-               None, functools.partial(text_pair, u))
+               None, functools.partial(text_pair, u), pair_ref)
         for u in range(3)
     ]
 
@@ -662,6 +669,8 @@
             pltpu.VMEM((3, 2, SEQ, 256), BF),
             pltpu.VMEM((3, SEQ, 256), F32),
             pltpu.VMEM((2, SEQ, 256), F32),
+            pltpu.VMEM((2, TOK, 512), F32),
+            pltpu.VMEM((2, TOK, 256), F32),
             pltpu.VMEM((32, 16, 256), BF),
             pltpu.VMEM((32, 16, 256), BF),
             pltpu.VMEM((32, 16, 128), BF),

time: 117 us -> 117 us (level)
  no operation moved by 1% of the time
where the time goes in v8:
time: 117 us
  Pallas kernels  112 us (96%)
  local copies, waits for them, and re-layouts  3.39 us (3%)
    pallas_call x1, Pallas kernels, per_device(): pl.pallas_call(kernel, out_shape=jax.ShapeDtypeStruct((SEQ, 512), BF), in...  112 us

profile of v8, /device:TPU:8, one launch (start us, length us, event | category | flops | bytes accessed | tf_op | source)
XLA Modules:
  0.0 117.3 jit_solution(3960120200367175928)
XLA Ops:
  0.0 0.0 copy-start.6
  0.0 0.8 fusion
  0.8 0.1 reshape.23
  0.9 0.2 copy.16
  1.1 0.1 copy.17
  1.2 0.0 copy-done.6
  1.2 0.2 reshape.25
  1.4 0.0 copy-start.7
  1.5 0.0 copy-start.8
  1.5 0.0 copy-start.4
  1.5 0.0 copy-start
  1.5 0.8 copy-done.7
  2.4 0.1 reshape.21
  2.5 0.2 copy.14
  2.7 0.0 copy-start.3
  2.7 0.1 copy.15
  2.9 0.0 copy-start.1
  2.9 0.0 copy-start.2
  2.9 0.0 copy-done.8
  3.7 0.0 copy-start.5
  3.7 0.0 copy-done.4
  3.7 0.0 copy-done
  3.7 0.0 copy-done.3
  3.7 0.1 copy-done.1
  3.8 0.1 copy-done.2
  3.9 0.5 copy-done.5
  4.4 112.2 %step.1 = bf16[384,512]{1,0:T(8,128)(2,1)S(1)} custom-call(s32[32]{0:T(128)S(1)} %copy-done.5, s32[1]{0:T(128)S(6)} %copy.26.off_ref, bf16[4,64,256]{2,1,0:T(8,128)(2,1)S(1)} %pad.12.vis_ref, f32[2,4,1,256]{3,2,1,0:T(1,128)S(1)} %pad.13.affine_ref, bf16[2,208,512]{2,1,0:T(8,128)(2,1)S(1)} %bitcast.21, bf16[256,512]{1,0:T(8,128)(2,1)S(1)} %copy-done.1, ...), custom_call_target="tpu_custom_call" | custom-call | tf_op jit(solution)/shard_map/step/pallas_call | solution.py:632
  116.6 0.7 copy.27
  (5 shorter events, 0.1 us)
Async XLA Ops:
  0.0 1.2 %copy-start.6 = (bf16[100,2,1024]{2,1,0:T(2,128)(2,1)S(1)}, bf16[100,2,1024]{2,1,0:T(2,128)(2,1)}, u32[]{:S(2)}) copy-start(bf16[100,2,1024]{2,1,0:T(2,128)(2,1)} %param.15) | copy-start | bytes 1228804
  1.4 0.9 copy-start.7
  1.5 1.4 %copy-start.8 = (bf16[256,2,128]{2,1,0:T(2,128)(2,1)S(1)}, bf16[256,2,128]{2,1,0:T(2,128)(2,1)}, u32[]{:S(2)}) copy-start(bf16[256,2,128]{2,1,0:T(2,128)(2,1)} %param.19) | copy-start | bytes 393220
  1.5 2.2 %copy-start.4 = (f32[8192]{0:T(1024)S(1)}, f32[8192]{0:T(1024)}, u32[]{:S(2)}) copy-start(f32[8192]{0:T(1024)} %param.17) | copy-start | bytes 98308
  1.5 2.2 %copy-start = (bf16[1,384,1024]{2,1,0:T(8,128)(2,1)S(1)}, bf16[1,384,1024]{2,1,0:T(8,128)(2,1)}, u32[]{:S(2)}) copy-start(bf16[1,384,1024]{2,1,0:T(8,128)(2,1)} %param.16) | copy-start | bytes 2359300
  2.7 1.0 copy-start.3
  2.9 1.0 copy-start.1
  2.9 1.0 copy-start.2
  3.7 0.7 copy-start.5
